TPU v7x, 32 devices: a whole 2x2x4 slice. The times are simulated.
32 devices in a mesh: blk: 16 (over z, x, core), head: 2 (over y).
Axes of the slice: x: 2, y: 2, z: 4, core: 2. Of those that a mesh axis runs over, the one named last changes fastest.
Arguments:
- query: bfloat16 [2, 8192, 128], P('head', 'blk'), may hold values from -12 to 12
- key: bfloat16 [8192, 128], P('blk'), may hold values from -6 to 6
- value: bfloat16 [8192, 128], P('blk'), may hold values from -6 to 6
- output: bfloat16 [2, 8192, 128], P('head', 'blk'), may hold values from -6 to 6
- out_grad: bfloat16 [2, 8192, 128], P('head', 'blk'), may hold values from -6 to 6
- lse: float32 [2, 8192], P('head', 'blk'), may hold values from 5 to 14
- block_order: int32 [32], replicated, may hold values from 0 to 31, as said below
Outputs:
- grad_query: float32 [2, 8192, 128], P('head', 'blk')
- grad_key: float32 [8192, 128], P(('blk', 'head'))
- grad_value: float32 [8192, 128], P(('blk', 'head'))
Inputs may be any that keep to these rules, and one draw needn't show every extreme that they name: A permutation of 0 to 31; the storage block j, rows j * 256 to (j + 1) * 256 - 1, holds the sequence block block_order[j].
All inputs are finite; a program needn't handle non-finite values.
Results may differ from a plain program's by a relative error of at most 0.0036.
Values may be sent and summed in bfloat16 or wider, within the bound.
No kernel may reach another device: no remote copies, remote signals or barrier semaphores. Data moves between devices by JAX's collectives and lax.ppermute only.
A program may use at most 64 MiB of HBM per device.

v0:
```python
import jax
import jax.numpy as jnp
from jax import lax
from jax.sharding import PartitionSpec as P


def passed_along(block, axis, distance):
    devices = range(lax.axis_size(axis))
    route = [((i - distance) % len(devices), i) for i in devices]
    return lax.ppermute(block, axis, route)


def inner(left, right):
    return lax.dot_general(
        left, right, (((1,), (1,)), ((), ())), preferred_element_type=jnp.float32
    )


def outer(left, right):
    return lax.dot_general(
        left, right, (((0,), (0,)), ((), ())), preferred_element_type=jnp.float32
    )


def tile_grads(q_rows, g_rows, l_rows, d_rows, q_pos, key, value, k_pos, scale):
    scores = inner(q_rows, key) * scale
    live = q_pos[:, None] >= k_pos[None, :]
    probs = jnp.where(live, jnp.exp(scores - l_rows[:, None]), 0.0)
    probs_low = probs.astype(jnp.bfloat16)
    dprobs = inner(g_rows, value)
    dscores = (probs * (dprobs - d_rows[:, None])).astype(jnp.bfloat16)
    grad_q = jnp.dot(dscores, key, preferred_element_type=jnp.float32) * scale
    grad_k = outer(dscores, q_rows) * scale
    grad_v = outer(probs_low, g_rows)
    return (grad_q, grad_k, grad_v)


def on_device(query, key, value, output, out_grad, lse, block_order):
    scale = key.shape[1] ** (-0.5)
    rows = key.shape[0]
    half = rows // 2
    devices = lax.axis_size("blk")
    mine = lax.axis_index("blk")
    q_rows = query[0]
    g_rows = out_grad[0]
    l_rows = lse[0]
    d_rows = jnp.sum(g_rows.astype(jnp.float32) * output[0].astype(jnp.float32), axis=1)
    offsets = jnp.arange(half, dtype=jnp.int32)

    def place(block):
        return lax.dynamic_index_in_dim(block_order, block, 0, keepdims=False) * half + offsets

    k_pos = jnp.concatenate([place(2 * mine), place(2 * mine + 1)])
    zeros = jnp.zeros(key.shape, jnp.float32)

    def visit(q_vis, g_vis, l_vis, d_vis, q_pos, grad_k, grad_v):
        part_q, part_k, part_v = tile_grads(
            q_vis, g_vis, l_vis, d_vis, q_pos, key, value, k_pos, scale
        )
        return (part_q, grad_k + part_k, grad_v + part_v)

    def turn(step, carry):
        q_vis, g_vis, dq_vis, l_vis, d_vis, grad_k, grad_v = carry
        source = (mine - step) % devices
        q_pos = jnp.concatenate([place(2 * source), place(2 * source + 1)])
        part_q, grad_k, grad_v = visit(q_vis, g_vis, l_vis, d_vis, q_pos, grad_k, grad_v)
        q_vis, g_vis = passed_along((q_vis, g_vis), "blk", 1)
        dq_vis, l_vis, d_vis = passed_along((dq_vis + part_q, l_vis, d_vis), "blk", 1)
        return (q_vis, g_vis, dq_vis, l_vis, d_vis, grad_k, grad_v)

    start = (q_rows, g_rows, zeros, l_rows, d_rows, zeros, zeros)
    final = lax.fori_loop(0, devices, turn, start)
    grad_q = final[2]
    grad_k = final[5]
    grad_v = final[6]
    own_k, own_v = (
        lax.psum_scatter(grad_k, "head", scatter_dimension=0, tiled=True),
        lax.psum_scatter(grad_v, "head", scatter_dimension=0, tiled=True),
    )
    return (grad_q[None], own_k, own_v)


def solution(mesh):
    in_specs = (
        P("head", "blk", None),
        P("blk", None),
        P("blk", None),
        P("head", "blk", None),
        P("head", "blk", None),
        P("head", "blk"),
        P(),
    )
    out_specs = (P("head", "blk", None), P(("blk", "head"), None), P(("blk", "head"), None))
    return jax.shard_map(
        on_device, mesh=mesh, in_specs=in_specs, out_specs=out_specs, check_vma=False
    )
```

profile of v0, /device:TPU:0, one launch (start us, length us, event | category | flops | bytes accessed | tf_op | source)
XLA Modules:
  0.0 259.9 jit_solution(3671025792148934461)
XLA Ops:
  11.9 212.9 %while.29 = (s32[]{:T(128)}, bf16[512,128]{1,0:T(8,128)(2,1)S(1)}, bf16[512,128]{1,0:T(8,128)(2,1)S(1)}, f32[512,128]{1,0:T(8,128)S(1)}, f32[512]{0:T(512)S(1)},...) while((s32[]{:T(128)}, bf16[512,128]{1,0:T(8,128)(2,1)S(1)}, ...), condition=%wide.region_2.3_spmd.clone.clone, body=%wide.region_1.2_spmd.clone.clone.sunk | while | flops 338101280 | bytes 9869981 | solution.py:72
  12.4 2.6 collective-permute-start.4
  15.1 1.7 collective-permute-start.1
  23.6 4.7 %collective-permute-done.2 = f32[512,128]{1,0:T(8,128)S(1)} collective-permute-done((f32[512,128]{1,0:T(8,128)S(1)}, f32[512,128]{1,0:T(8,128)S(1)}, u32[]{:S(2)}, u32[]{:S(2)}) %collective-permute-start.2) | collective-permute-done | bytes 262176 | tf_op jit(solution)/shard_map/while/body/eval_jaxpr/ppermute | solution.py:10
  36.9 4.5 %collective-permute-done.2 = f32[512,128]{1,0:T(8,128)S(1)} collective-permute-done((f32[512,128]{1,0:T(8,128)S(1)}, f32[512,128]{1,0:T(8,128)S(1)}, u32[]{:S(2)}, u32[]{:S(2)}) %collective-permute-start.2) | collective-permute-done | bytes 262176 | tf_op jit(solution)/shard_map/while/body/eval_jaxpr/ppermute | solution.py:10
  50.0 4.5 %collective-permute-done.2 = f32[512,128]{1,0:T(8,128)S(1)} collective-permute-done((f32[512,128]{1,0:T(8,128)S(1)}, f32[512,128]{1,0:T(8,128)S(1)}, u32[]{:S(2)}, u32[]{:S(2)}) %collective-permute-start.2) | collective-permute-done | bytes 262176 | tf_op jit(solution)/shard_map/while/body/eval_jaxpr/ppermute | solution.py:10
  63.1 3.1 %collective-permute-done.2 = f32[512,128]{1,0:T(8,128)S(1)} collective-permute-done((f32[512,128]{1,0:T(8,128)S(1)}, f32[512,128]{1,0:T(8,128)S(1)}, u32[]{:S(2)}, u32[]{:S(2)}) %collective-permute-start.2) | collective-permute-done | bytes 262176 | tf_op jit(solution)/shard_map/while/body/eval_jaxpr/ppermute | solution.py:10
  66.4 3.2 %collective-permute-start.1 = (bf16[512,128]{1,0:T(8,128)(2,1)S(1)}, bf16[512,128]{1,0:T(8,128)(2,1)S(1)}, u32[]{:S(2)}, u32[]{:S(2)}) collective-permute-start(bf16[512,128]{1,0:T(8,128)(2,1)S(1)} %copy.20), channel_id=1, source_target_pairs={{30,0},{0,2},{2,4},{4,6},{6,8},{8,10},{10,12},{12,14},{14,16},{16,... | collective-permute-start | bytes 393224 | tf_op jit(solution)/shard_map/while/body/eval_jaxpr/ppermute | solution.py:10
  74.9 6.2 %collective-permute-done.2 = f32[512,128]{1,0:T(8,128)S(1)} collective-permute-done((f32[512,128]{1,0:T(8,128)S(1)}, f32[512,128]{1,0:T(8,128)S(1)}, u32[]{:S(2)}, u32[]{:S(2)}) %collective-permute-start.2) | collective-permute-done | bytes 262176 | tf_op jit(solution)/shard_map/while/body/eval_jaxpr/ppermute | solution.py:10
  89.8 4.5 %collective-permute-done.2 = f32[512,128]{1,0:T(8,128)S(1)} collective-permute-done((f32[512,128]{1,0:T(8,128)S(1)}, f32[512,128]{1,0:T(8,128)S(1)}, u32[]{:S(2)}, u32[]{:S(2)}) %collective-permute-start.2) | collective-permute-done | bytes 262176 | tf_op jit(solution)/shard_map/while/body/eval_jaxpr/ppermute | solution.py:10
  102.9 4.5 %collective-permute-done.2 = f32[512,128]{1,0:T(8,128)S(1)} collective-permute-done((f32[512,128]{1,0:T(8,128)S(1)}, f32[512,128]{1,0:T(8,128)S(1)}, u32[]{:S(2)}, u32[]{:S(2)}) %collective-permute-start.2) | collective-permute-done | bytes 262176 | tf_op jit(solution)/shard_map/while/body/eval_jaxpr/ppermute | solution.py:10
  116.0 3.1 %collective-permute-done.2 = f32[512,128]{1,0:T(8,128)S(1)} collective-permute-done((f32[512,128]{1,0:T(8,128)S(1)}, f32[512,128]{1,0:T(8,128)S(1)}, u32[]{:S(2)}, u32[]{:S(2)}) %collective-permute-start.2) | collective-permute-done | bytes 262176 | tf_op jit(solution)/shard_map/while/body/eval_jaxpr/ppermute | solution.py:10
  119.3 3.2 %collective-permute-start.1 = (bf16[512,128]{1,0:T(8,128)(2,1)S(1)}, bf16[512,128]{1,0:T(8,128)(2,1)S(1)}, u32[]{:S(2)}, u32[]{:S(2)}) collective-permute-start(bf16[512,128]{1,0:T(8,128)(2,1)S(1)} %copy.20), channel_id=1, source_target_pairs={{30,0},{0,2},{2,4},{4,6},{6,8},{8,10},{10,12},{12,14},{14,16},{16,... | collective-permute-start | bytes 393224 | tf_op jit(solution)/shard_map/while/body/eval_jaxpr/ppermute | solution.py:10
  127.8 6.2 %collective-permute-done.2 = f32[512,128]{1,0:T(8,128)S(1)} collective-permute-done((f32[512,128]{1,0:T(8,128)S(1)}, f32[512,128]{1,0:T(8,128)S(1)}, u32[]{:S(2)}, u32[]{:S(2)}) %collective-permute-start.2) | collective-permute-done | bytes 262176 | tf_op jit(solution)/shard_map/while/body/eval_jaxpr/ppermute | solution.py:10
  142.6 4.5 %collective-permute-done.2 = f32[512,128]{1,0:T(8,128)S(1)} collective-permute-done((f32[512,128]{1,0:T(8,128)S(1)}, f32[512,128]{1,0:T(8,128)S(1)}, u32[]{:S(2)}, u32[]{:S(2)}) %collective-permute-start.2) | collective-permute-done | bytes 262176 | tf_op jit(solution)/shard_map/while/body/eval_jaxpr/ppermute | solution.py:10
  155.7 4.5 %collective-permute-done.2 = f32[512,128]{1,0:T(8,128)S(1)} collective-permute-done((f32[512,128]{1,0:T(8,128)S(1)}, f32[512,128]{1,0:T(8,128)S(1)}, u32[]{:S(2)}, u32[]{:S(2)}) %collective-permute-start.2) | collective-permute-done | bytes 262176 | tf_op jit(solution)/shard_map/while/body/eval_jaxpr/ppermute | solution.py:10
  168.8 3.1 %collective-permute-done.2 = f32[512,128]{1,0:T(8,128)S(1)} collective-permute-done((f32[512,128]{1,0:T(8,128)S(1)}, f32[512,128]{1,0:T(8,128)S(1)}, u32[]{:S(2)}, u32[]{:S(2)}) %collective-permute-start.2) | collective-permute-done | bytes 262176 | tf_op jit(solution)/shard_map/while/body/eval_jaxpr/ppermute | solution.py:10
  172.1 3.2 %collective-permute-start.1 = (bf16[512,128]{1,0:T(8,128)(2,1)S(1)}, bf16[512,128]{1,0:T(8,128)(2,1)S(1)}, u32[]{:S(2)}, u32[]{:S(2)}) collective-permute-start(bf16[512,128]{1,0:T(8,128)(2,1)S(1)} %copy.20), channel_id=1, source_target_pairs={{30,0},{0,2},{2,4},{4,6},{6,8},{8,10},{10,12},{12,14},{14,16},{16,... | collective-permute-start | bytes 393224 | tf_op jit(solution)/shard_map/while/body/eval_jaxpr/ppermute | solution.py:10
  180.6 6.2 %collective-permute-done.2 = f32[512,128]{1,0:T(8,128)S(1)} collective-permute-done((f32[512,128]{1,0:T(8,128)S(1)}, f32[512,128]{1,0:T(8,128)S(1)}, u32[]{:S(2)}, u32[]{:S(2)}) %collective-permute-start.2) | collective-permute-done | bytes 262176 | tf_op jit(solution)/shard_map/while/body/eval_jaxpr/ppermute | solution.py:10
  195.5 4.5 %collective-permute-done.2 = f32[512,128]{1,0:T(8,128)S(1)} collective-permute-done((f32[512,128]{1,0:T(8,128)S(1)}, f32[512,128]{1,0:T(8,128)S(1)}, u32[]{:S(2)}, u32[]{:S(2)}) %collective-permute-start.2) | collective-permute-done | bytes 262176 | tf_op jit(solution)/shard_map/while/body/eval_jaxpr/ppermute | solution.py:10
  208.6 4.5 %collective-permute-done.2 = f32[512,128]{1,0:T(8,128)S(1)} collective-permute-done((f32[512,128]{1,0:T(8,128)S(1)}, f32[512,128]{1,0:T(8,128)S(1)}, u32[]{:S(2)}, u32[]{:S(2)}) %collective-permute-start.2) | collective-permute-done | bytes 262176 | tf_op jit(solution)/shard_map/while/body/eval_jaxpr/ppermute | solution.py:10
  221.7 3.1 %collective-permute-done.2 = f32[512,128]{1,0:T(8,128)S(1)} collective-permute-done((f32[512,128]{1,0:T(8,128)S(1)}, f32[512,128]{1,0:T(8,128)S(1)}, u32[]{:S(2)}, u32[]{:S(2)}) %collective-permute-start.2) | collective-permute-done | bytes 262176 | tf_op jit(solution)/shard_map/while/body/eval_jaxpr/ppermute | solution.py:10
  226.3 11.5 %reduce-scatter.3.cloned.1.call-done = f32[256,128]{1,0:T(8,128)} async-done(((f32[512,128]{1,0:T(8,128)}), f32[256,128]{1,0:T(8,128)}) %reduce-scatter.3.cloned.1.call-update) | async-done | bytes 131088 | tf_op jit(solution)/shard_map/reduce_scatter | solution.py:77
  237.8 14.6 %reduce-scatter.5.cloned.1.call-done = f32[256,128]{1,0:T(8,128)} async-done(((f32[512,128]{1,0:T(8,128)}), f32[256,128]{1,0:T(8,128)}) %reduce-scatter.5.cloned.1.call-update) | async-done | bytes 131088 | tf_op jit(solution)/shard_map/reduce_scatter | solution.py:78
  (360 shorter events, 110.9 us)
Async XLA Ops:
  7.2 230.6 %reduce-scatter.3.cloned.1.call-start = ((), (), s32[]{:S(2)}) async-start(), calls=%async_computation.2 | async-start | bytes 393216 | tf_op jit(solution)/shard_map/reduce_scatter | solution.py:77
  11.9 8.7 %collective-permute-start.3 = (f32[512]{0:T(512)S(1)}, f32[512]{0:T(512)S(1)}, u32[]{:S(2)}, u32[]{:S(2)}) collective-permute-start(f32[512]{0:T(512)S(1)} %copy.22), channel_id=1, source_target_pairs={{30,0},{0,2},{2,4},{4,6},{6,8},{8,10},{10,12},{12,14},{14,16},{16,... | collective-permute-start | bytes 6152 | tf_op jit(solution)/shard_map/while/body/eval_jaxpr/ppermute | solution.py:10
  19.8 8.5 %collective-permute-start.2 = (f32[512,128]{1,0:T(8,128)S(1)}, f32[512,128]{1,0:T(8,128)S(1)}, u32[]{:S(2)}, u32[]{:S(2)}) collective-permute-start(f32[512,128]{1,0:T(8,128)S(1)} %fusion.50), channel_id=1, source_target_pairs={{30,0},{0,2},{2,4},{4,6},{6,8},{8,10},{10,12},{12,14},{14,16},{16,... | collective-permute-start | bytes 786440 | tf_op jit(solution)/shard_map/while/body/eval_jaxpr/ppermute | solution.py:10
  28.5 8.5 %collective-permute-start.1 = (bf16[512,128]{1,0:T(8,128)(2,1)S(1)}, bf16[512,128]{1,0:T(8,128)(2,1)S(1)}, u32[]{:S(2)}, u32[]{:S(2)}) collective-permute-start(bf16[512,128]{1,0:T(8,128)(2,1)S(1)} %copy.20), channel_id=1, source_target_pairs={{30,0},{0,2},{2,4},{4,6},{6,8},{8,10},{10,12},{12,14},{14,16},{16,... | collective-permute-start | bytes 393224 | tf_op jit(solution)/shard_map/while/body/eval_jaxpr/ppermute | solution.py:10
  32.9 8.5 %collective-permute-start.2 = (f32[512,128]{1,0:T(8,128)S(1)}, f32[512,128]{1,0:T(8,128)S(1)}, u32[]{:S(2)}, u32[]{:S(2)}) collective-permute-start(f32[512,128]{1,0:T(8,128)S(1)} %fusion.50), channel_id=1, source_target_pairs={{30,0},{0,2},{2,4},{4,6},{6,8},{8,10},{10,12},{12,14},{14,16},{16,... | collective-permute-start | bytes 786440 | tf_op jit(solution)/shard_map/while/body/eval_jaxpr/ppermute | solution.py:10
  46.0 8.5 %collective-permute-start.2 = (f32[512,128]{1,0:T(8,128)S(1)}, f32[512,128]{1,0:T(8,128)S(1)}, u32[]{:S(2)}, u32[]{:S(2)}) collective-permute-start(f32[512,128]{1,0:T(8,128)S(1)} %fusion.50), channel_id=1, source_target_pairs={{30,0},{0,2},{2,4},{4,6},{6,8},{8,10},{10,12},{12,14},{14,16},{16,... | collective-permute-start | bytes 786440 | tf_op jit(solution)/shard_map/while/body/eval_jaxpr/ppermute | solution.py:10
  57.7 8.5 %collective-permute-start.2 = (f32[512,128]{1,0:T(8,128)S(1)}, f32[512,128]{1,0:T(8,128)S(1)}, u32[]{:S(2)}, u32[]{:S(2)}) collective-permute-start(f32[512,128]{1,0:T(8,128)S(1)} %fusion.50), channel_id=1, source_target_pairs={{30,0},{0,2},{2,4},{4,6},{6,8},{8,10},{10,12},{12,14},{14,16},{16,... | collective-permute-start | bytes 786440 | tf_op jit(solution)/shard_map/while/body/eval_jaxpr/ppermute | solution.py:10
  72.6 8.5 %collective-permute-start.2 = (f32[512,128]{1,0:T(8,128)S(1)}, f32[512,128]{1,0:T(8,128)S(1)}, u32[]{:S(2)}, u32[]{:S(2)}) collective-permute-start(f32[512,128]{1,0:T(8,128)S(1)} %fusion.50), channel_id=1, source_target_pairs={{30,0},{0,2},{2,4},{4,6},{6,8},{8,10},{10,12},{12,14},{14,16},{16,... | collective-permute-start | bytes 786440 | tf_op jit(solution)/shard_map/while/body/eval_jaxpr/ppermute | solution.py:10
  85.7 8.5 %collective-permute-start.2 = (f32[512,128]{1,0:T(8,128)S(1)}, f32[512,128]{1,0:T(8,128)S(1)}, u32[]{:S(2)}, u32[]{:S(2)}) collective-permute-start(f32[512,128]{1,0:T(8,128)S(1)} %fusion.50), channel_id=1, source_target_pairs={{30,0},{0,2},{2,4},{4,6},{6,8},{8,10},{10,12},{12,14},{14,16},{16,... | collective-permute-start | bytes 786440 | tf_op jit(solution)/shard_map/while/body/eval_jaxpr/ppermute | solution.py:10
  98.8 8.5 %collective-permute-start.2 = (f32[512,128]{1,0:T(8,128)S(1)}, f32[512,128]{1,0:T(8,128)S(1)}, u32[]{:S(2)}, u32[]{:S(2)}) collective-permute-start(f32[512,128]{1,0:T(8,128)S(1)} %fusion.50), channel_id=1, source_target_pairs={{30,0},{0,2},{2,4},{4,6},{6,8},{8,10},{10,12},{12,14},{14,16},{16,... | collective-permute-start | bytes 786440 | tf_op jit(solution)/shard_map/while/body/eval_jaxpr/ppermute | solution.py:10
  110.6 8.5 %collective-permute-start.2 = (f32[512,128]{1,0:T(8,128)S(1)}, f32[512,128]{1,0:T(8,128)S(1)}, u32[]{:S(2)}, u32[]{:S(2)}) collective-permute-start(f32[512,128]{1,0:T(8,128)S(1)} %fusion.50), channel_id=1, source_target_pairs={{30,0},{0,2},{2,4},{4,6},{6,8},{8,10},{10,12},{12,14},{14,16},{16,... | collective-permute-start | bytes 786440 | tf_op jit(solution)/shard_map/while/body/eval_jaxpr/ppermute | solution.py:10
  119.3 8.5 %collective-permute-start.1 = (bf16[512,128]{1,0:T(8,128)(2,1)S(1)}, bf16[512,128]{1,0:T(8,128)(2,1)S(1)}, u32[]{:S(2)}, u32[]{:S(2)}) collective-permute-start(bf16[512,128]{1,0:T(8,128)(2,1)S(1)} %copy.20), channel_id=1, source_target_pairs={{30,0},{0,2},{2,4},{4,6},{6,8},{8,10},{10,12},{12,14},{14,16},{16,... | collective-permute-start | bytes 393224 | tf_op jit(solution)/shard_map/while/body/eval_jaxpr/ppermute | solution.py:10
  125.5 8.5 %collective-permute-start.2 = (f32[512,128]{1,0:T(8,128)S(1)}, f32[512,128]{1,0:T(8,128)S(1)}, u32[]{:S(2)}, u32[]{:S(2)}) collective-permute-start(f32[512,128]{1,0:T(8,128)S(1)} %fusion.50), channel_id=1, source_target_pairs={{30,0},{0,2},{2,4},{4,6},{6,8},{8,10},{10,12},{12,14},{14,16},{16,... | collective-permute-start | bytes 786440 | tf_op jit(solution)/shard_map/while/body/eval_jaxpr/ppermute | solution.py:10
  134.2 8.5 %collective-permute-start.1 = (bf16[512,128]{1,0:T(8,128)(2,1)S(1)}, bf16[512,128]{1,0:T(8,128)(2,1)S(1)}, u32[]{:S(2)}, u32[]{:S(2)}) collective-permute-start(bf16[512,128]{1,0:T(8,128)(2,1)S(1)} %copy.20), channel_id=1, source_target_pairs={{30,0},{0,2},{2,4},{4,6},{6,8},{8,10},{10,12},{12,14},{14,16},{16,... | collective-permute-start | bytes 393224 | tf_op jit(solution)/shard_map/while/body/eval_jaxpr/ppermute | solution.py:10
  138.6 8.5 %collective-permute-start.2 = (f32[512,128]{1,0:T(8,128)S(1)}, f32[512,128]{1,0:T(8,128)S(1)}, u32[]{:S(2)}, u32[]{:S(2)}) collective-permute-start(f32[512,128]{1,0:T(8,128)S(1)} %fusion.50), channel_id=1, source_target_pairs={{30,0},{0,2},{2,4},{4,6},{6,8},{8,10},{10,12},{12,14},{14,16},{16,... | collective-permute-start | bytes 786440 | tf_op jit(solution)/shard_map/while/body/eval_jaxpr/ppermute | solution.py:10
  147.3 8.5 %collective-permute-start.1 = (bf16[512,128]{1,0:T(8,128)(2,1)S(1)}, bf16[512,128]{1,0:T(8,128)(2,1)S(1)}, u32[]{:S(2)}, u32[]{:S(2)}) collective-permute-start(bf16[512,128]{1,0:T(8,128)(2,1)S(1)} %copy.20), channel_id=1, source_target_pairs={{30,0},{0,2},{2,4},{4,6},{6,8},{8,10},{10,12},{12,14},{14,16},{16,... | collective-permute-start | bytes 393224 | tf_op jit(solution)/shard_map/while/body/eval_jaxpr/ppermute | solution.py:10
  151.7 8.5 %collective-permute-start.2 = (f32[512,128]{1,0:T(8,128)S(1)}, f32[512,128]{1,0:T(8,128)S(1)}, u32[]{:S(2)}, u32[]{:S(2)}) collective-permute-start(f32[512,128]{1,0:T(8,128)S(1)} %fusion.50), channel_id=1, source_target_pairs={{30,0},{0,2},{2,4},{4,6},{6,8},{8,10},{10,12},{12,14},{14,16},{16,... | collective-permute-start | bytes 786440 | tf_op jit(solution)/shard_map/while/body/eval_jaxpr/ppermute | solution.py:10
  160.4 8.5 %collective-permute-start.1 = (bf16[512,128]{1,0:T(8,128)(2,1)S(1)}, bf16[512,128]{1,0:T(8,128)(2,1)S(1)}, u32[]{:S(2)}, u32[]{:S(2)}) collective-permute-start(bf16[512,128]{1,0:T(8,128)(2,1)S(1)} %copy.20), channel_id=1, source_target_pairs={{30,0},{0,2},{2,4},{4,6},{6,8},{8,10},{10,12},{12,14},{14,16},{16,... | collective-permute-start | bytes 393224 | tf_op jit(solution)/shard_map/while/body/eval_jaxpr/ppermute | solution.py:10
  163.4 8.5 %collective-permute-start.2 = (f32[512,128]{1,0:T(8,128)S(1)}, f32[512,128]{1,0:T(8,128)S(1)}, u32[]{:S(2)}, u32[]{:S(2)}) collective-permute-start(f32[512,128]{1,0:T(8,128)S(1)} %fusion.50), channel_id=1, source_target_pairs={{30,0},{0,2},{2,4},{4,6},{6,8},{8,10},{10,12},{12,14},{14,16},{16,... | collective-permute-start | bytes 786440 | tf_op jit(solution)/shard_map/while/body/eval_jaxpr/ppermute | solution.py:10
  178.3 8.5 %collective-permute-start.2 = (f32[512,128]{1,0:T(8,128)S(1)}, f32[512,128]{1,0:T(8,128)S(1)}, u32[]{:S(2)}, u32[]{:S(2)}) collective-permute-start(f32[512,128]{1,0:T(8,128)S(1)} %fusion.50), channel_id=1, source_target_pairs={{30,0},{0,2},{2,4},{4,6},{6,8},{8,10},{10,12},{12,14},{14,16},{16,... | collective-permute-start | bytes 786440 | tf_op jit(solution)/shard_map/while/body/eval_jaxpr/ppermute | solution.py:10
  191.4 8.5 %collective-permute-start.2 = (f32[512,128]{1,0:T(8,128)S(1)}, f32[512,128]{1,0:T(8,128)S(1)}, u32[]{:S(2)}, u32[]{:S(2)}) collective-permute-start(f32[512,128]{1,0:T(8,128)S(1)} %fusion.50), channel_id=1, source_target_pairs={{30,0},{0,2},{2,4},{4,6},{6,8},{8,10},{10,12},{12,14},{14,16},{16,... | collective-permute-start | bytes 786440 | tf_op jit(solution)/shard_map/while/body/eval_jaxpr/ppermute | solution.py:10
  204.5 8.5 %collective-permute-start.2 = (f32[512,128]{1,0:T(8,128)S(1)}, f32[512,128]{1,0:T(8,128)S(1)}, u32[]{:S(2)}, u32[]{:S(2)}) collective-permute-start(f32[512,128]{1,0:T(8,128)S(1)} %fusion.50), channel_id=1, source_target_pairs={{30,0},{0,2},{2,4},{4,6},{6,8},{8,10},{10,12},{12,14},{14,16},{16,... | collective-permute-start | bytes 786440 | tf_op jit(solution)/shard_map/while/body/eval_jaxpr/ppermute | solution.py:10
  216.3 8.5 %collective-permute-start.2 = (f32[512,128]{1,0:T(8,128)S(1)}, f32[512,128]{1,0:T(8,128)S(1)}, u32[]{:S(2)}, u32[]{:S(2)}) collective-permute-start(f32[512,128]{1,0:T(8,128)S(1)} %fusion.50), channel_id=1, source_target_pairs={{30,0},{0,2},{2,4},{4,6},{6,8},{8,10},{10,12},{12,14},{14,16},{16,... | collective-permute-start | bytes 786440 | tf_op jit(solution)/shard_map/while/body/eval_jaxpr/ppermute | solution.py:10
  225.6 26.8 %reduce-scatter.5.cloned.1.call-start = ((), (), s32[]{:S(2)}) async-start(), calls=%async_computation.3 | async-start | bytes 393216 | tf_op jit(solution)/shard_map/reduce_scatter | solution.py:78
  (66 other events, 405.0 us)
Sparse Core Ops, SparseCore 0:
  225.7 12.0 reduce-scatter.2
  240.6 11.7 reduce-scatter.4
where the time goes:
time: 260 us
  waiting for transfers between devices  149 us (57%)
  starting transfers between devices  29.7 us (11%)
  matrix products  28 us (11%)
  loops' own time  21.9 us (8%)
  local copies, waits for them, and re-layouts  15.4 us (6%)
  between operations  15.4 us (6%)
    ppermute x80, waiting for transfers between devices, passed_along(): return lax.ppermute(block, axis, route)  122 us
    ppermute x80, starting transfers between devices, passed_along(): return lax.ppermute(block, axis, route)  29.6 us
    another operation x1, loops' own time, on_device(): final = lax.fori_loop(0, devices, turn, start)  21.9 us
    reduce_scatter x1, waiting for transfers between devices, on_device(): lax.psum_scatter(grad_v, 'head', scatter_dimension=0, tiled=True)  14.6 us
    dot_general x32, matrix products, outer(): lax.dot_general(left, right, (((0,), (0,)), ((), ())), preferred_element_...  12.3 us
    reduce_scatter x1, waiting for transfers between devices, on_device(): lax.psum_scatter(grad_k, 'head', scatter_dimension=0, tiled=True)  11.5 us
    dynamic_slice x17, local copies, waits for them, and re-layouts, place(): lax.dynamic_index_in_dim(block_order, block, 0, keepdims=False) * half  11 us
    dot_general x32, matrix products, inner(): lax.dot_general(left, right, (((1,), (1,)), ((), ())), preferred_element_...  11 us
  transfers between devices with their start and end apart: 82, of which 71 were waited for; matrix products, arithmetic and copies ran while one was open for 15% of the time, Pallas kernels for 0%

commit v1 on v0

v1 whole, which is shorter than its diff:
```python
import functools

import jax
import jax.numpy as jnp
from jax import lax
from jax.experimental import pallas as pl
from jax.experimental.pallas import tpu as pltpu
from jax.sharding import PartitionSpec as P


LOG2E = 1.4426950408889634
WIDTH = 4
LIMIT = 24 * 2**20
VMEM = pl.BlockSpec(memory_space=pltpu.VMEM)
SMEM = pl.BlockSpec(memory_space=pltpu.SMEM)


def contract(left, right, dims):
    return lax.dot_general(left, right, (dims, ((), ())), preferred_element_type=jnp.float32)


def pieces_of(row):
    found = []
    for _ in range(3):
        piece = row.astype(jnp.bfloat16).astype(jnp.float32)
        found.append(piece)
        row = row - piece
    return found


def pack_kernel(split, *refs):
    given, (sent, kv_mine, kv_all), local, done = refs[:6], refs[6:9], refs[9:15], refs[15]
    copies = [pltpu.make_async_copy(a, b, done.at[n]) for n, (a, b) in enumerate(zip(given, local))]
    for copy in copies:
        copy.start()
    for copy in copies:
        copy.wait()
    k, v, q, g, o, low = local
    rows, width = q.shape
    block = rows // 2
    head = lax.axis_index("head")
    for part in range(2):
        half = lax.rem(head + part, 2) if split else part
        at = pl.ds(pl.multiple_of(half * block, block), block)
        kv_all[2 * part] = k[at, :]
        kv_all[2 * part + 1] = v[at, :]
        if part == 0:
            kv_mine[0] = k[at, :]
            kv_mine[1] = v[at, :]
    sent[:rows] = q[...]
    sent[rows : 2 * rows] = g[...]
    product = g[...].astype(jnp.float32) * o[...].astype(jnp.float32)
    delta = jnp.sum(product.T, axis=0, keepdims=True)
    lines = [
        piece[:, at : at + width]
        for row in (low[...] * LOG2E, delta)
        for piece in pieces_of(row)
        for at in range(0, rows, width)
    ]
    pad = sent.shape[0] - 2 * rows - len(lines)
    lines.append(jnp.zeros((pad, width), jnp.float32))
    sent[2 * rows :] = jnp.concatenate(lines, axis=0).astype(jnp.bfloat16)


def pack(query, output, out_grad, lse, key, value, split):
    rows, width = query.shape
    block = rows // 2
    lines = -(-6 * (rows // width) // 16) * 16
    given = (key, value, query, out_grad, output, lse)
    return pl.pallas_call(
        functools.partial(pack_kernel, split),
        out_shape=[
            jax.ShapeDtypeStruct((2 * rows + lines, width), jnp.bfloat16),
            jax.ShapeDtypeStruct((2, block, width), jnp.bfloat16),
            jax.ShapeDtypeStruct((4, block, width), jnp.bfloat16),
        ],
        in_specs=[pl.BlockSpec(memory_space=pltpu.HBM)] * len(given),
        out_specs=[VMEM] * 3,
        scratch_shapes=[pltpu.VMEM(a.shape, a.dtype) for a in given]
        + [pltpu.SemaphoreType.DMA((len(given),))],
        compiler_params=pltpu.CompilerParams(vmem_limit_bytes=LIMIT),
        name="pack",
    )(*[pltpu.with_memory_space_constraint(a, pltpu.HBM) for a in given])


def tile_kernel(shape, *refs):
    q_units, q_held, q_done, k_units, n_kv, k_held, k_done, split, rows, width, scale = shape
    block = rows // 2
    n_q, n_k = 2 * len(q_units), 2 * len(k_units)
    refs = list(refs)

    def take(count):
        taken, refs[:] = refs[:count], refs[count:]
        return taken

    (order,) = take(1)
    q_in, kv_in = take(len(q_units)), take(n_kv)
    q_before = dict(zip(q_held, take(len(q_held))))
    k_before = take(1)[0] if k_held else None
    dq_out = dict(zip(q_units, take(len(q_units))))
    sent, kept = take(2) if k_done else (None, take(1)[0])
    q, g, low, delta, k, v, kt, dqt, total, q_at, k_at, pair_q, pair_k = refs

    me = lax.axis_index("blk")
    head = lax.axis_index("head")
    lines = rows // width
    for u, offset in enumerate(q_units):
        stats = q_in[u][2 * rows :].astype(jnp.float32)
        for half in range(2):
            i = 2 * u + half
            q[i] = q_in[u][half * block : (half + 1) * block]
            g[i] = q_in[u][rows + half * block : rows + (half + 1) * block]
            for kind, out in enumerate((low, delta)):
                pieces = [
                    stats[(3 * kind + p) * lines : (3 * kind + p + 1) * lines] for p in range(3)
                ]
                row = pieces[0] + pieces[1] + pieces[2]
                start = half * (lines // 2)
                out[i] = jnp.concatenate(
                    [row[c : c + 1] for c in range(start, start + lines // 2)], axis=1
                )
            q_at[i] = order[2 * (me ^ offset) + half]
            if offset in q_before:
                dqt[i] = q_before[offset][half]
            else:
                dqt[i] = jnp.zeros((width, block), jnp.float32)
    blocks = [(ref, at) for ref in kv_in for at in range(0, ref.shape[0], 2)]
    for j, (ref, at) in enumerate(blocks):
        k[j] = ref[at]
        v[j] = ref[at + 1]
        kt[j] = ref[at].T
        half = lax.rem(head + j % 2, 2) if split else j % 2
        k_at[j] = order[2 * (me ^ k_units[j // 2]) + half]
    total[...] = k_before[...] if k_held else jnp.zeros_like(total)

    found = jnp.int32(0)
    for i in range(n_q):
        at = q_at[i]
        for j in range(n_k):
            pair_q[found] = jnp.int32(i)
            pair_k[found] = jnp.int32(j)
            found += (at >= k_at[j]).astype(jnp.int32)
    for e in range(WIDTH - 1):
        pair_q[found + e] = jnp.int32(0)
        pair_k[found + e] = jnp.int32(-1)

    ahead = lax.broadcasted_iota(jnp.int32, (block, block), 1) - lax.broadcasted_iota(
        jnp.int32, (block, block), 0
    )

    def each_group(t, _):
        at_q = [pair_q[t * WIDTH + e] for e in range(WIDTH)]
        named = [pair_k[t * WIDTH + e] for e in range(WIDTH)]
        at_k = [jnp.maximum(j, 0) for j in named]
        probs_low, dscores = [], []
        for i, j, name in zip(at_q, at_k, named):
            least = jnp.where(name < 0, 2 * block, (k_at[j] - q_at[i]) * block)
            scores = contract(k[j], q[i], ((1,), (1,)))
            dprobs = contract(v[j], g[i], ((1,), (1,)))
            probs = jnp.where(ahead >= least, jnp.exp2(scores * (scale * LOG2E) - low[i]), 0.0)
            probs_low.append(probs.astype(jnp.bfloat16))
            dscores.append((probs * (dprobs - delta[i])).astype(jnp.bfloat16))
        part_v = [contract(p, g[i], ((1,), (0,))) for p, i in zip(probs_low, at_q)]
        part_k = [contract(d, q[i], ((1,), (0,))) for d, i in zip(dscores, at_q)]
        part_q = [contract(kt[j], d, ((1,), (0,))) for d, j in zip(dscores, at_k)]
        for i, j, a, b, c in zip(at_q, at_k, part_k, part_v, part_q):
            total[2 * j] += a
            total[2 * j + 1] += b
            dqt[i] += c
        return 0

    lax.fori_loop(0, (found + WIDTH - 1) // WIDTH, each_group, 0)
    for u, offset in enumerate(q_units):
        out = dq_out[offset]
        for half in range(2):
            if offset in q_done:
                got = (dqt[2 * u + half] * scale).T.astype(out.dtype)
                out[half * block : (half + 1) * block] = got
            else:
                out[half] = dqt[2 * u + half]
    if k_done:
        place = {0: 0, 1: 0}
        for u, offset in enumerate(k_units):
            out = sent if offset & 1 else kept
            for j in (2 * u, 2 * u + 1):
                at = place[offset & 1]
                out[at] = (total[2 * j] * scale).astype(out.dtype)
                out[at + 1] = total[2 * j + 1].astype(out.dtype)
                place[offset & 1] = at + 2
    else:
        kept[...] = total[...]


def tile_grads(order, q, kv, q_before, k_before, q_done, k_done, split, rows, scale):
    q_units, k_units = tuple(q), tuple(kv)
    kv = [a for o in k_units for a in kv[o]]
    width = kv[0].shape[2]
    block = rows // 2
    n_q, n_k = 2 * len(q_units), 2 * len(k_units)
    out_shape = []
    for offset in q_units:
        if offset not in q_done:
            out_shape.append(jax.ShapeDtypeStruct((2, width, block), jnp.float32))
        else:
            kind = jnp.bfloat16 if offset else jnp.float32
            out_shape.append(jax.ShapeDtypeStruct((rows, width), kind))
    if k_done:
        out_shape.append(jax.ShapeDtypeStruct((n_k, block, width), jnp.bfloat16))
        out_shape.append(jax.ShapeDtypeStruct((n_k, block, width), jnp.float32))
    else:
        out_shape.append(jax.ShapeDtypeStruct((2 * n_k, block, width), jnp.float32))
    pairs = n_q * n_k // 2
    q_held = tuple(o for o in q_units if o in q_before)
    k_held = k_before is not None
    operands = [*q.values(), *kv, *(q_before[o] for o in q_held)] + ([k_before] if k_held else [])
    shape = (q_units, q_held, q_done, k_units, len(kv), k_held, k_done, split, rows, width, scale)
    outs = pl.pallas_call(
        functools.partial(tile_kernel, shape),
        out_shape=out_shape,
        in_specs=[SMEM] + [VMEM] * len(operands),
        out_specs=[VMEM] * len(out_shape),
        scratch_shapes=[
            pltpu.VMEM((n_q, block, width), jnp.bfloat16),
            pltpu.VMEM((n_q, block, width), jnp.bfloat16),
            pltpu.VMEM((n_q, 1, block), jnp.float32),
            pltpu.VMEM((n_q, 1, block), jnp.float32),
            pltpu.VMEM((n_k, block, width), jnp.bfloat16),
            pltpu.VMEM((n_k, block, width), jnp.bfloat16),
            pltpu.VMEM((n_k, width, block), jnp.bfloat16),
            pltpu.VMEM((n_q, width, block), jnp.float32),
            pltpu.VMEM((2 * n_k, block, width), jnp.float32),
            pltpu.SMEM((n_q,), jnp.int32),
            pltpu.SMEM((n_k,), jnp.int32),
            pltpu.SMEM((n_q * n_k + WIDTH,), jnp.int32),
            pltpu.SMEM((n_q * n_k + WIDTH,), jnp.int32),
        ],
        cost_estimate=pl.CostEstimate(
            flops=pairs * block * block * width * 10,
            bytes_accessed=(n_q + n_k) * block * width * 8,
            transcendentals=pairs * block * block,
        ),
        compiler_params=pltpu.CompilerParams(vmem_limit_bytes=LIMIT),
        name="tile_grads",
    )(order, *operands)
    return dict(zip(q_units, outs)), outs[len(q_units) :]


def offsets_of(bits):
    found = [0]
    for bit in bits:
        found = found + [o | 1 << bit for o in found]
    return tuple(sorted(found))


def share_kernel(places, kept, got, *outs):
    for out, (at, size) in zip(outs, places):
        if size == 1:
            out[...] = (kept[at] + got[at].astype(jnp.float32)).astype(out.dtype)
        else:
            for n in range(size):
                out[n] = (kept[at + n] + got[at + n].astype(jnp.float32)).astype(out.dtype)


def share(kept, got, kinds):
    size = kept.shape[0] // len(kinds)
    places, shapes = [], []
    for n, group in enumerate(kinds):
        each = size // len(group)
        for e, kind in enumerate(group):
            places.append((n * size + e * each, each))
            lead = kept.shape[1:] if each == 1 else (each,) + kept.shape[1:]
            shapes.append(jax.ShapeDtypeStruct(lead, kind))
    return pl.pallas_call(
        functools.partial(share_kernel, tuple(places)),
        out_shape=shapes,
        in_specs=[VMEM] * 2,
        out_specs=[VMEM] * len(shapes),
        compiler_params=pltpu.CompilerParams(vmem_limit_bytes=LIMIT),
        name="share",
    )(kept, got)


def on_device(query, key, value, output, out_grad, lse, block_order):
    rows, width = key.shape
    scale = width ** (-0.5)
    devices = lax.axis_size("blk")
    heads = lax.axis_size("head")
    bits = devices.bit_length() - 1
    q_bits = tuple(range(bits))[1:3]
    k_bits = tuple(b for b in range(bits) if b not in q_bits)
    q_units, k_units = offsets_of(q_bits), offsets_of(k_bits)
    split = heads == 2

    def across(array, offset):
        return lax.ppermute(array, "blk", [(i, i ^ offset) for i in range(devices)])

    def across_both(array, offset):
        route = [(2 * i + h, 2 * (i ^ offset) + 1 - h) for i in range(devices) for h in range(2)]
        return lax.ppermute(array, ("blk", "head"), route)

    sent, kv_mine, kv_all = pack(query[0], output[0], out_grad[0], lse, key, value, split)

    held = {0: [kv_all]}
    for bit in k_bits[:0:-1]:
        for o in list(held):
            if split and o == 0:
                mine = across(kv_mine, 1 << bit)
                held[1 << bit] = [mine, across_both(mine, 0)]
            else:
                far = [across(a, 1 << bit) for a in held[o]]
                held[o | 1 << bit] = far
    q = {o: across(sent, o) if o else sent for o in q_units}
    for o in list(held):
        held[o | 1] = [across(a, 1) for a in held[o]]

    def some(array_of, units):
        return {o: array_of[o] for o in units}

    home = [o for o in k_units if o < 2]
    away = [o for o in k_units if o >= 2]
    early, late = q_units[:-1], q_units[-1:]
    tile = functools.partial(tile_grads, block_order, split=split, rows=rows, scale=scale)
    held_q, (total,) = tile(some(q, early), some(held, home), {}, None, (), False)
    dq, (far_sent, far_kept) = tile(some(q, q_units), some(held, away), held_q, None, early, True)
    held_q = some(dq, late)
    far_got = across(far_sent, 1)
    last_q, (home_sent, home_kept) = tile(
        some(q, late), some(held, home), held_q, total, late, True
    )
    dq |= last_q
    home_got = across(home_sent, 1)

    low, wide = jnp.bfloat16, jnp.float32
    far_offsets = [o for o in away if not o & 1]
    arrived = []
    if split:
        far = share(far_kept, far_got, [(wide, low), (low, low)] * len(far_offsets))
        for n, offset in enumerate(far_offsets):
            (mine_k, mine_v), (other_k, other_v) = far[4 * n : 4 * n + 2], far[4 * n + 2 : 4 * n + 4]
            other_k = across_both(other_k, 0)
            both_k = (mine_k + other_k.astype(wide)).astype(low)
            arrived.append(
                ((across(both_k, offset),), (across_both(other_v, offset), across(mine_v, offset)))
            )
        own_k, own_v, *other = share(home_kept, home_got, [(wide, wide), (low,)])
        (other,) = other
        other = across_both(other, 0)
        own_k, own_v = own_k + other[0].astype(wide), own_v + other[1].astype(wide)
        for from_k, from_v in arrived:
            own_k = sum((a.astype(wide) for a in from_k), own_k)
            own_v = sum((a.astype(wide) for a in from_v), own_v)
    else:
        far = share(far_kept, far_got, [(low,)] * len(far_offsets))
        (own,) = share(home_kept, home_got, [(wide,)])
        for offset, array in zip(far_offsets, far):
            own = own + across(array, offset).astype(wide)
        own_k, own_v = (
            lax.psum_scatter(
                jnp.concatenate([own[t], own[2 + t]]), "head", scatter_dimension=0, tiled=True
            )
            for t in range(2)
        )
    grad_q = dq[0]
    for offset in q_units[1:]:
        grad_q = grad_q + across(dq[offset], offset).astype(jnp.float32)
    return (grad_q[None], own_k, own_v)


def solution(mesh):
    in_specs = (
        P("head", "blk", None),
        P("blk", None),
        P("blk", None),
        P("head", "blk", None),
        P("head", "blk", None),
        P("head", "blk"),
        P(),
    )
    out_specs = (P("head", "blk", None), P(("blk", "head"), None), P(("blk", "head"), None))

    def step(*args):
        return on_device(*args)

    step = jax.shard_map(
        step, mesh=mesh, in_specs=in_specs, out_specs=out_specs, check_vma=False
    )
    return step
```

time: 260 us -> 50.6 us (0.19)
  waiting for transfers between devices: 149 us -> 14.5 us
  matrix products: 28 us -> 0 us
  loops' own time: 21.9 us -> 0 us
  local copies, waits for them, and re-layouts: 15.4 us -> 0.01 us
  between operations: 15.4 us -> 0.72 us
  Pallas kernels: 0 us -> 11.9 us
  starting transfers between devices: 29.7 us -> 21.8 us
    ppermute x80 -> x18, waiting for transfers between devices: 122 us -> 14.5 us  [the longest x14 11.1 us: across(): return lax.ppermute(array, 'blk', [(i, i ^ offset) for i in range(devices)])]
    dot_general x80 -> x0, matrix products: 28 us -> none  [the longest x32 12.3 us: outer(): lax.dot_general(left, right, (((0,), (0,)), ((), ())), preferred_element_...]
    reduce_scatter x2 -> x0, waiting for transfers between devices: 26.1 us -> none  [the longest x1 14.6 us: on_device(): lax.psum_scatter(grad_v, 'head', scatter_dimension=0, tiled=True)]
    another operation x1 -> x0, loops' own time: 21.9 us -> none  [on_device(): final = lax.fori_loop(0, devices, turn, start)]
    pallas_call x0 -> x6, Pallas kernels: none -> 11.9 us  [the longest x3 10.4 us: tile_grads(): pl.pallas_call(functools.partial(tile_kernel, shape), out_shape=out_shape...]
    dynamic_slice x17 -> x0, local copies, waits for them, and re-layouts: 11 us -> none  [place(): lax.dynamic_index_in_dim(block_order, block, 0, keepdims=False) * half]
    ppermute x80 -> x18, starting transfers between devices: 29.6 us -> 21.8 us  [the longest x14 14.8 us: across(): return lax.ppermute(array, 'blk', [(i, i ^ offset) for i in range(devices)])]
    unnamed x18 -> x2, local copies, waits for them, and re-layouts: 3.96 us -> 0.01 us
  transfers between devices with their start and end apart: 82 -> 18, of which waited for: 71 -> 7; matrix products, arithmetic and copies ran while one was open for 15% -> 2% of each run, Pallas kernels for 0% -> 14%
where the time goes in v1:
time: 50.6 us; the launch traced here: 50.5 us
  starting transfers between devices  21.8 us (43%)
  waiting for transfers between devices  14.5 us (29%)
  Pallas kernels  11.9 us (24%)
  other arithmetic  1.54 us (3%)
  between operations  0.72 us (1%)
    ppermute x14, starting transfers between devices, across(): return lax.ppermute(array, 'blk', [(i, i ^ offset) for i in range(devices)])  14.8 us
    ppermute x14, waiting for transfers between devices, across(): return lax.ppermute(array, 'blk', [(i, i ^ offset) for i in range(devices)])  11.1 us
    pallas_call x3, Pallas kernels, tile_grads(): pl.pallas_call(functools.partial(tile_kernel, shape), out_shape=out_shape...  10.4 us
    ppermute x4, starting transfers between devices, across_both(): return lax.ppermute(array, ('blk', 'head'), route)  7.04 us
    ppermute x4, waiting for transfers between devices, across_both(): return lax.ppermute(array, ('blk', 'head'), route)  3.41 us
    pallas_call x1, Pallas kernels, pack(): pl.pallas_call(functools.partial(pack_kernel, split), out_shape=[jax.Shap...  1.42 us
  transfers between devices with their start and end apart: 18, of which 7 were waited for; matrix products, arithmetic and copies ran while one was open for 2% of the time, Pallas kernels for 14%

profile of v1, /device:TPU:0, one launch (start us, length us, event | category | flops | bytes accessed | tf_op | source)
XLA Modules:
  0.0 50.5 jit_solution(838772596541755563)
XLA Ops:
  0.6 1.4 %pack.1 = (bf16[1056,128]{1,0:T(8,128)(2,1)S(1)}, bf16[2,256,128]{2,1,0:T(8,128)(2,1)S(1)}, bf16[4,256,128]{2,1,0:T(8,128)(2,1)S(1)}) custom-call(bf16[512,128]{1,0:T(8,128)(2,1)} %refs_0_.4, bf16[512,128]{1,0:T(8,128)(2,1)} %refs_1_.1, bf16[512,128]{1,0:T(8,128)(2,1)} %bitcast.15, bf16[512,128]{1,0:T(8,128)(2,1)} %bitcast.16, bf16[512,128]{1,0:T(8,128)(2,1)} %bitcast.17, ...), custom_call_target="tpu_custom_call" | custom-call | tf_op jit(solution)/shard_map/pack/pallas_call | solution.py:70
  2.1 4.1 %collective-permute-start.3 = (bf16[2,256,128]{2,1,0:T(8,128)(2,1)S(1)}, bf16[2,256,128]{2,1,0:T(8,128)(2,1)S(1)}, u32[]{:S(2)}, u32[]{:S(2)}) collective-permute-start(bf16[2,256,128]{2,1,0:T(8,128)(2,1)S(1)} %get-tuple-element.27), channel_id=1, source_target_pairs={{0,16},{2,18},{4,20},{6,22},{8,24},{10,26},{12,28},{14,30},{16,0},... | collective-permute-start | bytes 393224 | tf_op jit(solution)/shard_map/ppermute | solution.py:295
  6.2 1.6 %collective-permute-start.1 = (bf16[1056,128]{1,0:T(8,128)(2,1)S(1)}, bf16[1056,128]{1,0:T(8,128)(2,1)S(1)}, u32[]{:S(2)}, u32[]{:S(2)}) collective-permute-start(bf16[1056,128]{1,0:T(8,128)(2,1)S(1)} %get-tuple-element.26.refs_1_), channel_id=1, source_target_pairs={{0,8},{2,10},{4,12},{6,14},{8,0},{10,2},{12,4},{14,6},{16,24},{18,... | collective-permute-start | bytes 811016 | tf_op jit(solution)/shard_map/ppermute | solution.py:295
  7.8 1.5 %collective-permute-start = (bf16[1056,128]{1,0:T(8,128)(2,1)S(1)}, bf16[1056,128]{1,0:T(8,128)(2,1)S(1)}, u32[]{:S(2)}, u32[]{:S(2)}) collective-permute-start(bf16[1056,128]{1,0:T(8,128)(2,1)S(1)} %get-tuple-element.26.refs_1_), channel_id=1, source_target_pairs={{0,4},{2,6},{4,0},{6,2},{8,12},{10,14},{12,8},{14,10},{16,20},{18,... | collective-permute-start | bytes 811016 | tf_op jit(solution)/shard_map/ppermute | solution.py:295
  9.7 2.9 %collective-permute-done.3.refs_5_ = bf16[2,256,128]{2,1,0:T(8,128)(2,1)S(1)} collective-permute-done((bf16[2,256,128]{2,1,0:T(8,128)(2,1)S(1)}, bf16[2,256,128]{2,1,0:T(8,128)(2,1)S(1)}, u32[]{:S(2)}, u32[]{:S(2)}) %collective-permute-start.3) | collective-permute-done | bytes 131104 | tf_op jit(solution)/shard_map/ppermute | solution.py:295
  12.6 1.6 %collective-permute-start.4 = (bf16[2,256,128]{2,1,0:T(8,128)(2,1)S(1)}, bf16[2,256,128]{2,1,0:T(8,128)(2,1)S(1)}, u32[]{:S(2)}, u32[]{:S(2)}) collective-permute-start(bf16[2,256,128]{2,1,0:T(8,128)(2,1)S(1)} %collective-permute-done.3.refs_5_), channel_id=1, source_target_pairs={{0,1},{1,0},{2,3},{3,2},{4,5},{5,4},{6,7},{7,6},{8,9},{9,8},{10,11... | collective-permute-start | bytes 393224 | tf_op jit(solution)/shard_map/ppermute | solution.py:299
  14.2 3.4 %collective-permute-done.4.refs_6_ = bf16[2,256,128]{2,1,0:T(8,128)(2,1)S(1)} collective-permute-done((bf16[2,256,128]{2,1,0:T(8,128)(2,1)S(1)}, bf16[2,256,128]{2,1,0:T(8,128)(2,1)S(1)}, u32[]{:S(2)}, u32[]{:S(2)}) %collective-permute-start.4) | collective-permute-done | bytes 131104 | tf_op jit(solution)/shard_map/ppermute | solution.py:299
  18.1 4.3 %tile_grads.3 = (f32[2,128,256]{2,1,0:T(8,128)S(1)}, f32[2,128,256]{2,1,0:T(8,128)S(1)}, f32[2,128,256]{2,1,0:T(8,128)S(1)}, f32[8,256,128]{2,1,0:T(8,128)S(1)}) custom-call(s32[32]{0:T(128)S(1)} %copy-done, bf16[1056,128]{1,0:T(8,128)(2,1)S(1)} %get-tuple-element.26.refs_1_, bf16[1056,128]{1,0:T(8,128)(2,1)S(1)} %collective-permute-done.refs_2_, ...), custom_call_target="tpu_custom_call" | custom-call | flops 1006632960 | bytes 2621440 | tf_op jit(solution)/shard_map/tile_grads/pallas_call | solution.py:217
  22.4 1.1 %collective-permute-done.2.refs_4_.refs_1_ = bf16[1056,128]{1,0:T(8,128)(2,1)S(1)} collective-permute-done((bf16[1056,128]{1,0:T(8,128)(2,1)S(1)}, bf16[1056,128]{1,0:T(8,128)(2,1)S(1)}, u32[]{:S(2)}, u32[]{:S(2)}) %collective-permute-start.2) | collective-permute-done | bytes 270368 | tf_op jit(solution)/shard_map/ppermute | solution.py:295
  23.5 3.6 %tile_grads.4 = (f32[512,128]{1,0:T(8,128)S(1)}, bf16[512,128]{1,0:T(8,128)(2,1)S(1)}, bf16[512,128]{1,0:T(8,128)(2,1)S(1)}, f32[2,128,256]{2,1,0:T(8,128)S(1)},...) custom-call(s32[32]{0:T(128)S(1)} %copy-done, bf16[1056,128]{1,0:T(8,128)(2,1)S(1)} %get-tuple-element.26.refs_1_, ...), custom_call_target="tpu_custom_call" | custom-call | flops 1342177280 | bytes 3145728 | tf_op jit(solution)/shard_map/tile_grads/pallas_call | solution.py:217
  27.2 2.5 %tile_grads.5 = (bf16[512,128]{1,0:T(8,128)(2,1)S(1)}, bf16[4,256,128]{2,1,0:T(8,128)(2,1)S(1)}, f32[4,256,128]{2,1,0:T(8,128)S(1)}) custom-call(s32[32]{0:T(128)S(1)} %copy-done, bf16[1056,128]{1,0:T(8,128)(2,1)S(1)} %collective-permute-done.2.refs_4_.refs_1_, bf16[4,256,128]{2,1,0:T(8,128)(2,1)S(1)} %get-tuple-element.28.refs_4_.refs_2_, ...), custom_call_target="tpu_custom_call" | custom-call | flops 335544320 | bytes 1572864 | tf_op jit(solution)/shard_map/tile_grads/pallas_call | solution.py:217
  29.7 0.6 %collective-permute-start.11 = (bf16[4,256,128]{2,1,0:T(8,128)(2,1)S(1)}, bf16[4,256,128]{2,1,0:T(8,128)(2,1)S(1)}, u32[]{:S(2)}, u32[]{:S(2)}) collective-permute-start(bf16[4,256,128]{2,1,0:T(8,128)(2,1)S(1)} %get-tuple-element.39), channel_id=1, source_target_pairs={{0,2},{2,0},{4,6},{6,4},{8,10},{10,8},{12,14},{14,12},{16,18},{18,... | collective-permute-start | bytes 786440 | tf_op jit(solution)/shard_map/ppermute | solution.py:295
  30.3 1.6 %collective-permute-start.14 = (bf16[256,128]{1,0:T(8,128)(2,1)S(1)}, bf16[256,128]{1,0:T(8,128)(2,1)S(1)}, u32[]{:S(2)}, u32[]{:S(2)}) collective-permute-start(bf16[256,128]{1,0:T(8,128)(2,1)S(1)} %get-tuple-element.45), channel_id=1, source_target_pairs={{0,1},{1,0},{2,3},{3,2},{4,5},{5,4},{6,7},{7,6},{8,9},{9,8},{10,11... | collective-permute-start | bytes 196616 | tf_op jit(solution)/shard_map/ppermute | solution.py:299
  31.9 2.5 %collective-permute-start.8 = (bf16[512,128]{1,0:T(8,128)(2,1)S(1)}, bf16[512,128]{1,0:T(8,128)(2,1)S(1)}, u32[]{:S(2)}, u32[]{:S(2)}) collective-permute-start(bf16[512,128]{1,0:T(8,128)(2,1)S(1)} %get-tuple-element.33), channel_id=1, source_target_pairs={{0,4},{2,6},{4,0},{6,2},{8,12},{10,14},{12,8},{14,10},{16,20},{18,... | collective-permute-start | bytes 393224 | tf_op jit(solution)/shard_map/ppermute | solution.py:295
  34.5 1.5 %collective-permute-start.10 = (bf16[512,128]{1,0:T(8,128)(2,1)S(1)}, bf16[512,128]{1,0:T(8,128)(2,1)S(1)}, u32[]{:S(2)}, u32[]{:S(2)}) collective-permute-start(bf16[512,128]{1,0:T(8,128)(2,1)S(1)} %get-tuple-element.37), channel_id=1, source_target_pairs={{0,12},{2,14},{4,8},{6,10},{8,4},{10,6},{12,0},{14,2},{16,28},{18,... | collective-permute-start | bytes 393224 | tf_op jit(solution)/shard_map/ppermute | solution.py:295
  36.0 0.6 %collective-permute-start.12 = (bf16[2,256,128]{2,1,0:T(8,128)(2,1)S(1)}, bf16[2,256,128]{2,1,0:T(8,128)(2,1)S(1)}, u32[]{:S(2)}, u32[]{:S(2)}) collective-permute-start(bf16[2,256,128]{2,1,0:T(8,128)(2,1)S(1)} %get-tuple-element.41), channel_id=1, source_target_pairs={{0,1},{1,0},{2,3},{3,2},{4,5},{5,4},{6,7},{7,6},{8,9},{9,8},{10,11... | collective-permute-start | bytes 393224 | tf_op jit(solution)/shard_map/ppermute | solution.py:299
  36.5 3.3 %collective-permute-start.16 = (bf16[256,128]{1,0:T(8,128)(2,1)S(1)}, bf16[256,128]{1,0:T(8,128)(2,1)S(1)}, u32[]{:S(2)}, u32[]{:S(2)}) collective-permute-start(bf16[256,128]{1,0:T(8,128)(2,1)S(1)} %get-tuple-element.47), channel_id=1, source_target_pairs={{0,17},{1,16},{2,19},{3,18},{4,21},{5,20},{6,23},{7,22},{8,25},{9,... | collective-permute-start | bytes 196616 | tf_op jit(solution)/shard_map/ppermute | solution.py:299
  39.9 0.6 %collective-permute-start.17 = (bf16[256,128]{1,0:T(8,128)(2,1)S(1)}, bf16[256,128]{1,0:T(8,128)(2,1)S(1)}, u32[]{:S(2)}, u32[]{:S(2)}) collective-permute-start(bf16[256,128]{1,0:T(8,128)(2,1)S(1)} %get-tuple-element.48), channel_id=1, source_target_pairs={{0,16},{2,18},{4,20},{6,22},{8,24},{10,26},{12,28},{14,30},{16,0},... | collective-permute-start | bytes 196616 | tf_op jit(solution)/shard_map/ppermute | solution.py:295
  40.5 1.0 %collective-permute-done.9 = bf16[512,128]{1,0:T(8,128)(2,1)S(1)} collective-permute-done((bf16[512,128]{1,0:T(8,128)(2,1)S(1)}, bf16[512,128]{1,0:T(8,128)(2,1)S(1)}, u32[]{:S(2)}, u32[]{:S(2)}) %collective-permute-start.9) | collective-permute-done | bytes 131104 | tf_op jit(solution)/shard_map/ppermute | solution.py:295
  41.5 1.4 %collective-permute-start.15 = (bf16[256,128]{1,0:T(8,128)(2,1)S(1)}, bf16[256,128]{1,0:T(8,128)(2,1)S(1)}, u32[]{:S(2)}, u32[]{:S(2)}) collective-permute-start(bf16[256,128]{1,0:T(8,128)(2,1)S(1)} %add_convert_fusion), channel_id=1, source_target_pairs={{0,16},{2,18},{4,20},{6,22},{8,24},{10,26},{12,28},{14,30},{16,0},... | collective-permute-start | bytes 196616 | tf_op jit(solution)/shard_map/ppermute | solution.py:295
  43.0 0.8 %add_bitcast_fusion = f32[1,512,128]{2,1,0:T(8,128)} fusion(bf16[512,128]{1,0:T(8,128)(2,1)S(1)} %collective-permute-done.10, bf16[512,128]{1,0:T(8,128)(2,1)S(1)} %collective-permute-done.9, f32[512,128]{1,0:T(8,128)S(1)} %get-tuple-element.32, bf16[512,128]{1,0:T(8,128)(2,1)S(1)} %collective-permute-done.8), kind=kLoop, calls=%fused_computation | loop fusion | flops 393216 | bytes 917504 | tf_op jit(solution)/shard_map/broadcast_in_dim | solution.py:366
  43.8 5.2 %collective-permute-done.17 = bf16[256,128]{1,0:T(8,128)(2,1)S(1)} collective-permute-done((bf16[256,128]{1,0:T(8,128)(2,1)S(1)}, bf16[256,128]{1,0:T(8,128)(2,1)S(1)}, u32[]{:S(2)}, u32[]{:S(2)}) %collective-permute-start.17) | collective-permute-done | bytes 65568 | tf_op jit(solution)/shard_map/ppermute | solution.py:295
  49.0 0.7 %collective-permute-done.15 = bf16[256,128]{1,0:T(8,128)(2,1)S(1)} collective-permute-done((bf16[256,128]{1,0:T(8,128)(2,1)S(1)}, bf16[256,128]{1,0:T(8,128)(2,1)S(1)}, u32[]{:S(2)}, u32[]{:S(2)}) %collective-permute-start.15) | collective-permute-done | bytes 65568 | tf_op jit(solution)/shard_map/ppermute | solution.py:295
  49.7 0.7 %fusion.1 = (f32[256,128]{1,0:T(8,128)}, f32[256,128]{1,0:T(8,128)}) fusion(f32[256,128]{1,0:T(8,128)S(1)} %get-tuple-element.46, bf16[256,128]{1,0:T(8,128)(2,1)S(1)} %collective-permute-done.17, bf16[256,128]{1,0:T(8,128)(2,1)S(1)} %collective-permute-done.16, bf16[2,256,128]{2,1,0:T(8,128)(2,1)S(1)} %collective-permute-done.12, ...), kind=kLoop, calls=%fused_computation.3 | loop fusion | flops 327680 | bytes 851968 | tf_op jit(solution)/shard_map/add | solution.py:351
  (23 shorter events, 1.3 us)
Async XLA Ops:
  2.1 10.5 %collective-permute-start.3 = (bf16[2,256,128]{2,1,0:T(8,128)(2,1)S(1)}, bf16[2,256,128]{2,1,0:T(8,128)(2,1)S(1)}, u32[]{:S(2)}, u32[]{:S(2)}) collective-permute-start(bf16[2,256,128]{2,1,0:T(8,128)(2,1)S(1)} %get-tuple-element.27), channel_id=1, source_target_pairs={{0,16},{2,18},{4,20},{6,22},{8,24},{10,26},{12,28},{14,30},{16,0},... | collective-permute-start | bytes 393224 | tf_op jit(solution)/shard_map/ppermute | solution.py:295
  6.2 11.9 %copy-start = (s32[32]{0:T(128)S(1)}, s32[32]{0:T(128)}, u32[]{:S(2)}) copy-start(s32[32]{0:T(128)} %refs_0_.7) | copy-start | bytes 388
  6.2 11.4 %collective-permute-start.7 = (bf16[4,256,128]{2,1,0:T(8,128)(2,1)S(1)}, bf16[4,256,128]{2,1,0:T(8,128)(2,1)S(1)}, u32[]{:S(2)}, u32[]{:S(2)}) collective-permute-start(bf16[4,256,128]{2,1,0:T(8,128)(2,1)S(1)} %get-tuple-element.28.refs_4_.refs_2_), channel_id=1, source_target_pairs={{0,2},{2,0},{4,6},{6,4},{8,10},{10,8},{12,14},{14,12},{16,18},{18,... | collective-permute-start | bytes 786440 | tf_op jit(solution)/shard_map/ppermute | solution.py:295
  6.2 11.9 %collective-permute-start.1 = (bf16[1056,128]{1,0:T(8,128)(2,1)S(1)}, bf16[1056,128]{1,0:T(8,128)(2,1)S(1)}, u32[]{:S(2)}, u32[]{:S(2)}) collective-permute-start(bf16[1056,128]{1,0:T(8,128)(2,1)S(1)} %get-tuple-element.26.refs_1_), channel_id=1, source_target_pairs={{0,8},{2,10},{4,12},{6,14},{8,0},{10,2},{12,4},{14,6},{16,24},{18,... | collective-permute-start | bytes 811016 | tf_op jit(solution)/shard_map/ppermute | solution.py:295
  7.8 10.3 %collective-permute-start = (bf16[1056,128]{1,0:T(8,128)(2,1)S(1)}, bf16[1056,128]{1,0:T(8,128)(2,1)S(1)}, u32[]{:S(2)}, u32[]{:S(2)}) collective-permute-start(bf16[1056,128]{1,0:T(8,128)(2,1)S(1)} %get-tuple-element.26.refs_1_), channel_id=1, source_target_pairs={{0,4},{2,6},{4,0},{6,2},{8,12},{10,14},{12,8},{14,10},{16,20},{18,... | collective-permute-start | bytes 811016 | tf_op jit(solution)/shard_map/ppermute | solution.py:295
  9.3 14.2 %collective-permute-start.2 = (bf16[1056,128]{1,0:T(8,128)(2,1)S(1)}, bf16[1056,128]{1,0:T(8,128)(2,1)S(1)}, u32[]{:S(2)}, u32[]{:S(2)}) collective-permute-start(bf16[1056,128]{1,0:T(8,128)(2,1)S(1)} %get-tuple-element.26.refs_1_), channel_id=1, source_target_pairs={{0,12},{2,14},{4,8},{6,10},{8,4},{10,6},{12,0},{14,2},{16,28},{18,... | collective-permute-start | bytes 811016 | tf_op jit(solution)/shard_map/ppermute | solution.py:295
  12.6 5.0 %collective-permute-start.4 = (bf16[2,256,128]{2,1,0:T(8,128)(2,1)S(1)}, bf16[2,256,128]{2,1,0:T(8,128)(2,1)S(1)}, u32[]{:S(2)}, u32[]{:S(2)}) collective-permute-start(bf16[2,256,128]{2,1,0:T(8,128)(2,1)S(1)} %collective-permute-done.3.refs_5_), channel_id=1, source_target_pairs={{0,1},{1,0},{2,3},{3,2},{4,5},{5,4},{6,7},{7,6},{8,9},{9,8},{10,11... | collective-permute-start | bytes 393224 | tf_op jit(solution)/shard_map/ppermute | solution.py:299
  17.6 4.8 %collective-permute-start.5 = (bf16[2,256,128]{2,1,0:T(8,128)(2,1)S(1)}, bf16[2,256,128]{2,1,0:T(8,128)(2,1)S(1)}, u32[]{:S(2)}, u32[]{:S(2)}) collective-permute-start(bf16[2,256,128]{2,1,0:T(8,128)(2,1)S(1)} %collective-permute-done.3.refs_5_), channel_id=1, source_target_pairs={{0,2},{2,0},{4,6},{6,4},{8,10},{10,8},{12,14},{14,12},{16,18},{18,... | collective-permute-start | bytes 393224 | tf_op jit(solution)/shard_map/ppermute | solution.py:295
  17.6 5.9 %collective-permute-start.6 = (bf16[2,256,128]{2,1,0:T(8,128)(2,1)S(1)}, bf16[2,256,128]{2,1,0:T(8,128)(2,1)S(1)}, u32[]{:S(2)}, u32[]{:S(2)}) collective-permute-start(bf16[2,256,128]{2,1,0:T(8,128)(2,1)S(1)} %collective-permute-done.4.refs_6_), channel_id=1, source_target_pairs={{0,2},{2,0},{4,6},{6,4},{8,10},{10,8},{12,14},{14,12},{16,18},{18,... | collective-permute-start | bytes 393224 | tf_op jit(solution)/shard_map/ppermute | solution.py:295
  27.1 3.2 %collective-permute-start.13 = (bf16[4,256,128]{2,1,0:T(8,128)(2,1)S(1)}, bf16[4,256,128]{2,1,0:T(8,128)(2,1)S(1)}, u32[]{:S(2)}, u32[]{:S(2)}) collective-permute-start(bf16[4,256,128]{2,1,0:T(8,128)(2,1)S(1)} %get-tuple-element.43), channel_id=1, source_target_pairs={{0,2},{2,0},{4,6},{6,4},{8,10},{10,8},{12,14},{14,12},{16,18},{18,... | collective-permute-start | bytes 786440 | tf_op jit(solution)/shard_map/ppermute | solution.py:295
  29.7 6.2 %collective-permute-start.11 = (bf16[4,256,128]{2,1,0:T(8,128)(2,1)S(1)}, bf16[4,256,128]{2,1,0:T(8,128)(2,1)S(1)}, u32[]{:S(2)}, u32[]{:S(2)}) collective-permute-start(bf16[4,256,128]{2,1,0:T(8,128)(2,1)S(1)} %get-tuple-element.39), channel_id=1, source_target_pairs={{0,2},{2,0},{4,6},{6,4},{8,10},{10,8},{12,14},{14,12},{16,18},{18,... | collective-permute-start | bytes 786440 | tf_op jit(solution)/shard_map/ppermute | solution.py:295
  30.3 6.2 %collective-permute-start.14 = (bf16[256,128]{1,0:T(8,128)(2,1)S(1)}, bf16[256,128]{1,0:T(8,128)(2,1)S(1)}, u32[]{:S(2)}, u32[]{:S(2)}) collective-permute-start(bf16[256,128]{1,0:T(8,128)(2,1)S(1)} %get-tuple-element.45), channel_id=1, source_target_pairs={{0,1},{1,0},{2,3},{3,2},{4,5},{5,4},{6,7},{7,6},{8,9},{9,8},{10,11... | collective-permute-start | bytes 196616 | tf_op jit(solution)/shard_map/ppermute | solution.py:299
  31.9 8.0 %collective-permute-start.8 = (bf16[512,128]{1,0:T(8,128)(2,1)S(1)}, bf16[512,128]{1,0:T(8,128)(2,1)S(1)}, u32[]{:S(2)}, u32[]{:S(2)}) collective-permute-start(bf16[512,128]{1,0:T(8,128)(2,1)S(1)} %get-tuple-element.33), channel_id=1, source_target_pairs={{0,4},{2,6},{4,0},{6,2},{8,12},{10,14},{12,8},{14,10},{16,20},{18,... | collective-permute-start | bytes 393224 | tf_op jit(solution)/shard_map/ppermute | solution.py:295
  34.5 7.1 %collective-permute-start.9 = (bf16[512,128]{1,0:T(8,128)(2,1)S(1)}, bf16[512,128]{1,0:T(8,128)(2,1)S(1)}, u32[]{:S(2)}, u32[]{:S(2)}) collective-permute-start(bf16[512,128]{1,0:T(8,128)(2,1)S(1)} %get-tuple-element.34), channel_id=1, source_target_pairs={{0,8},{2,10},{4,12},{6,14},{8,0},{10,2},{12,4},{14,6},{16,24},{18,... | collective-permute-start | bytes 393224 | tf_op jit(solution)/shard_map/ppermute | solution.py:295
  34.5 8.6 %collective-permute-start.10 = (bf16[512,128]{1,0:T(8,128)(2,1)S(1)}, bf16[512,128]{1,0:T(8,128)(2,1)S(1)}, u32[]{:S(2)}, u32[]{:S(2)}) collective-permute-start(bf16[512,128]{1,0:T(8,128)(2,1)S(1)} %get-tuple-element.37), channel_id=1, source_target_pairs={{0,12},{2,14},{4,8},{6,10},{8,4},{10,6},{12,0},{14,2},{16,28},{18,... | collective-permute-start | bytes 393224 | tf_op jit(solution)/shard_map/ppermute | solution.py:295
  36.0 13.8 %collective-permute-start.12 = (bf16[2,256,128]{2,1,0:T(8,128)(2,1)S(1)}, bf16[2,256,128]{2,1,0:T(8,128)(2,1)S(1)}, u32[]{:S(2)}, u32[]{:S(2)}) collective-permute-start(bf16[2,256,128]{2,1,0:T(8,128)(2,1)S(1)} %get-tuple-element.41), channel_id=1, source_target_pairs={{0,1},{1,0},{2,3},{3,2},{4,5},{5,4},{6,7},{7,6},{8,9},{9,8},{10,11... | collective-permute-start | bytes 393224 | tf_op jit(solution)/shard_map/ppermute | solution.py:299
  36.5 7.2 %collective-permute-start.16 = (bf16[256,128]{1,0:T(8,128)(2,1)S(1)}, bf16[256,128]{1,0:T(8,128)(2,1)S(1)}, u32[]{:S(2)}, u32[]{:S(2)}) collective-permute-start(bf16[256,128]{1,0:T(8,128)(2,1)S(1)} %get-tuple-element.47), channel_id=1, source_target_pairs={{0,17},{1,16},{2,19},{3,18},{4,21},{5,20},{6,23},{7,22},{8,25},{9,... | collective-permute-start | bytes 196616 | tf_op jit(solution)/shard_map/ppermute | solution.py:299
  39.9 9.1 %collective-permute-start.17 = (bf16[256,128]{1,0:T(8,128)(2,1)S(1)}, bf16[256,128]{1,0:T(8,128)(2,1)S(1)}, u32[]{:S(2)}, u32[]{:S(2)}) collective-permute-start(bf16[256,128]{1,0:T(8,128)(2,1)S(1)} %get-tuple-element.48), channel_id=1, source_target_pairs={{0,16},{2,18},{4,20},{6,22},{8,24},{10,26},{12,28},{14,30},{16,0},... | collective-permute-start | bytes 196616 | tf_op jit(solution)/shard_map/ppermute | solution.py:295
  41.5 8.2 %collective-permute-start.15 = (bf16[256,128]{1,0:T(8,128)(2,1)S(1)}, bf16[256,128]{1,0:T(8,128)(2,1)S(1)}, u32[]{:S(2)}, u32[]{:S(2)}) collective-permute-start(bf16[256,128]{1,0:T(8,128)(2,1)S(1)} %add_convert_fusion), channel_id=1, source_target_pairs={{0,16},{2,18},{4,20},{6,22},{8,24},{10,26},{12,28},{14,30},{16,0},... | collective-permute-start | bytes 196616 | tf_op jit(solution)/shard_map/ppermute | solution.py:295

commit v2 on v1

--- a/solution.py
+++ b/solution.py
@@ -84,9 +84,9 @@
 
 
 def tile_kernel(shape, *refs):
-    q_units, q_held, q_done, k_units, n_kv, k_held, k_done, split, rows, width, scale = shape
+    q_units, q_held, q_done, blocks, n_kv, k_held, k_done, skip, split, rows, width, scale = shape
     block = rows // 2
-    n_q, n_k = 2 * len(q_units), 2 * len(k_units)
+    n_q, n_k = 2 * len(q_units), len(blocks)
     refs = list(refs)
 
     def take(count):
@@ -124,19 +124,25 @@
                 dqt[i] = q_before[offset][half]
             else:
                 dqt[i] = jnp.zeros((width, block), jnp.float32)
-    blocks = [(ref, at) for ref in kv_in for at in range(0, ref.shape[0], 2)]
-    for j, (ref, at) in enumerate(blocks):
+    pieces = [(ref, at) for ref in kv_in for at in range(0, ref.shape[0], 2)]
+    for j, ((ref, at), (offset, part)) in enumerate(zip(pieces, blocks)):
         k[j] = ref[at]
         v[j] = ref[at + 1]
         kt[j] = ref[at].T
-        half = lax.rem(head + j % 2, 2) if split else j % 2
-        k_at[j] = order[2 * (me ^ k_units[j // 2]) + half]
-    total[...] = k_before[...] if k_held else jnp.zeros_like(total)
+        half = lax.rem(head + part, 2) if split else part
+        k_at[j] = order[2 * (me ^ offset) + half]
+        for t in range(2):
+            if blocks[j] in k_held:
+                total[2 * j + t] = k_before[2 * k_held.index(blocks[j]) + t]
+            else:
+                total[2 * j + t] = jnp.zeros((block, width), jnp.float32)
 
     found = jnp.int32(0)
     for i in range(n_q):
         at = q_at[i]
         for j in range(n_k):
+            if (q_units[i // 2], blocks[j]) in skip:
+                continue
             pair_q[found] = jnp.int32(i)
             pair_k[found] = jnp.int32(j)
             found += (at >= k_at[j]).astype(jnp.int32)
@@ -152,21 +158,25 @@
         at_q = [pair_q[t * WIDTH + e] for e in range(WIDTH)]
         named = [pair_k[t * WIDTH + e] for e in range(WIDTH)]
         at_k = [jnp.maximum(j, 0) for j in named]
-        probs_low, dscores = [], []
-        for i, j, name in zip(at_q, at_k, named):
-            least = jnp.where(name < 0, 2 * block, (k_at[j] - q_at[i]) * block)
+
+        def front(e):
+            i, j = at_q[e], at_k[e]
+            least = jnp.where(named[e] < 0, 2 * block, (k_at[j] - q_at[i]) * block)
             scores = contract(k[j], q[i], ((1,), (1,)))
             dprobs = contract(v[j], g[i], ((1,), (1,)))
             probs = jnp.where(ahead >= least, jnp.exp2(scores * (scale * LOG2E) - low[i]), 0.0)
-            probs_low.append(probs.astype(jnp.bfloat16))
-            dscores.append((probs * (dprobs - delta[i])).astype(jnp.bfloat16))
-        part_v = [contract(p, g[i], ((1,), (0,))) for p, i in zip(probs_low, at_q)]
-        part_k = [contract(d, q[i], ((1,), (0,))) for d, i in zip(dscores, at_q)]
-        part_q = [contract(kt[j], d, ((1,), (0,))) for d, j in zip(dscores, at_k)]
-        for i, j, a, b, c in zip(at_q, at_k, part_k, part_v, part_q):
-            total[2 * j] += a
-            total[2 * j + 1] += b
-            dqt[i] += c
+            dscores = (probs * (dprobs - delta[i])).astype(jnp.bfloat16)
+            return probs.astype(jnp.bfloat16), dscores
+
+        ready = front(0)
+        for e in range(WIDTH):
+            probs_low, dscores = ready
+            if e + 1 < WIDTH:
+                ready = front(e + 1)
+            i, j = at_q[e], at_k[e]
+            total[2 * j + 1] += contract(probs_low, g[i], ((1,), (0,)))
+            total[2 * j] += contract(dscores, q[i], ((1,), (0,)))
+            dqt[i] += contract(kt[j], dscores, ((1,), (0,)))
         return 0
 
     lax.fori_loop(0, (found + WIDTH - 1) // WIDTH, each_group, 0)
@@ -180,23 +190,31 @@
                 out[half] = dqt[2 * u + half]
     if k_done:
         place = {0: 0, 1: 0}
-        for u, offset in enumerate(k_units):
-            out = sent if offset & 1 else kept
-            for j in (2 * u, 2 * u + 1):
-                at = place[offset & 1]
-                out[at] = (total[2 * j] * scale).astype(out.dtype)
-                out[at + 1] = total[2 * j + 1].astype(out.dtype)
-                place[offset & 1] = at + 2
+        for j, (offset, _) in enumerate(blocks):
+            out, at = sent if offset & 1 else kept, place[offset & 1]
+            out[at] = (total[2 * j] * scale).astype(out.dtype)
+            out[at + 1] = total[2 * j + 1].astype(out.dtype)
+            place[offset & 1] = at + 2
     else:
         kept[...] = total[...]
 
 
-def tile_grads(order, q, kv, q_before, k_before, q_done, k_done, split, rows, scale):
-    q_units, k_units = tuple(q), tuple(kv)
-    kv = [a for o in k_units for a in kv[o]]
+def blocks_of(kv):
+    found = []
+    for offset, arrays in kv.items():
+        count = sum(a.shape[0] // 2 for a in arrays)
+        found += [(offset, part) for part in range(count)]
+    return tuple(found)
+
+
+def tile_grads(
+    order, q, kv, q_before, k_before, q_done, k_done, split, rows, scale, skip=frozenset()
+):
+    q_units, blocks = tuple(q), blocks_of(kv)
+    kv = [a for arrays in kv.values() for a in arrays]
     width = kv[0].shape[2]
     block = rows // 2
-    n_q, n_k = 2 * len(q_units), 2 * len(k_units)
+    n_q, n_k = 2 * len(q_units), len(blocks)
     out_shape = []
     for offset in q_units:
         if offset not in q_done:
@@ -211,9 +229,9 @@
         out_shape.append(jax.ShapeDtypeStruct((2 * n_k, block, width), jnp.float32))
     pairs = n_q * n_k // 2
     q_held = tuple(o for o in q_units if o in q_before)
-    k_held = k_before is not None
+    k_held, k_before = k_before or ((), None)
     operands = [*q.values(), *kv, *(q_before[o] for o in q_held)] + ([k_before] if k_held else [])
-    shape = (q_units, q_held, q_done, k_units, len(kv), k_held, k_done, split, rows, width, scale)
+    shape = (q_units, q_held, q_done, blocks, len(kv), k_held, k_done, skip, split, rows, width, scale)
     outs = pl.pallas_call(
         functools.partial(tile_kernel, shape),
         out_shape=out_shape,
@@ -318,37 +336,46 @@
 
     home = [o for o in k_units if o < 2]
     away = [o for o in k_units if o >= 2]
-    early, late = q_units[:-1], q_units[-1:]
+    mine, near, late = q_units[:1], q_units[1:-1], q_units[-1:]
     tile = functools.partial(tile_grads, block_order, split=split, rows=rows, scale=scale)
-    held_q, (total,) = tile(some(q, early), some(held, home), {}, None, (), False)
-    dq, (far_sent, far_kept) = tile(some(q, q_units), some(held, away), held_q, None, early, True)
+    home_kv, away_kv = some(held, home), some(held, away)
+    home_blocks = blocks_of(home_kv)
+    held_q, (total,) = tile(some(q, mine), home_kv, {}, None, (), False)
+    if split:
+        first_kv = {o: arrays[:1] for o, arrays in away_kv.items()}
+        first = q_units[:2]
+        first_blocks = blocks_of(first_kv)
+        more_q, (away_total,) = tile(some(q, first), first_kv, held_q, None, (), False)
+        held_q |= more_q
+        away_before = (first_blocks, away_total)
+        skip = frozenset((o, at) for o in first for at in first_blocks)
+    else:
+        away_before, skip = None, frozenset()
+    more_q, (total,) = tile(
+        some(q, near), home_kv, some(held_q, held_q.keys() & near), (home_blocks, total), (), False
+    )
+    held_q |= more_q
+    dq, (far_sent, far_kept) = tile(
+        some(q, q_units), away_kv, held_q, away_before, mine + near, True, skip=skip
+    )
     held_q = some(dq, late)
     far_got = across(far_sent, 1)
     last_q, (home_sent, home_kept) = tile(
-        some(q, late), some(held, home), held_q, total, late, True
+        some(q, late), home_kv, held_q, (home_blocks, total), late, True
     )
     dq |= last_q
     home_got = across(home_sent, 1)
 
     low, wide = jnp.bfloat16, jnp.float32
     far_offsets = [o for o in away if not o & 1]
-    arrived = []
     if split:
-        far = share(far_kept, far_got, [(wide, low), (low, low)] * len(far_offsets))
-        for n, offset in enumerate(far_offsets):
-            (mine_k, mine_v), (other_k, other_v) = far[4 * n : 4 * n + 2], far[4 * n + 2 : 4 * n + 4]
-            other_k = across_both(other_k, 0)
-            both_k = (mine_k + other_k.astype(wide)).astype(low)
-            arrived.append(
-                ((across(both_k, offset),), (across_both(other_v, offset), across(mine_v, offset)))
-            )
-        own_k, own_v, *other = share(home_kept, home_got, [(wide, wide), (low,)])
-        (other,) = other
-        other = across_both(other, 0)
-        own_k, own_v = own_k + other[0].astype(wide), own_v + other[1].astype(wide)
-        for from_k, from_v in arrived:
-            own_k = sum((a.astype(wide) for a in from_k), own_k)
-            own_v = sum((a.astype(wide) for a in from_v), own_v)
+        far = share(far_kept, far_got, [(wide,), (low,)] * len(far_offsets))
+        own, other = share(home_kept, home_got, [(wide,), (low,)])
+        own = own + across_both(other, 0).astype(wide)
+        for offset, kept, sent in zip(far_offsets, far[::2], far[1::2]):
+            both = kept + across_both(sent, 0).astype(wide)
+            own = own + across(both.astype(low), offset).astype(wide)
+        own_k, own_v = own[0], own[1]
     else:
         far = share(far_kept, far_got, [(low,)] * len(far_offsets))
         (own,) = share(home_kept, home_got, [(wide,)])

time: 50.6 us -> 49.2 us (0.972)
  waiting for transfers between devices: 14.5 us -> 10.9 us
  Pallas kernels: 11.9 us -> 14.8 us
  other arithmetic: 1.54 us -> 0.83 us
  local copies, waits for them, and re-layouts: 0.01 us -> 0.72 us
  starting transfers between devices: 21.8 us -> 21.1 us
    ppermute x4 -> x3, starting transfers between devices: 7.04 us -> 2.96 us  [across_both(): return lax.ppermute(array, ('blk', 'head'), route)]
    ppermute x14 -> x13, starting transfers between devices: 14.8 us -> 18.1 us  [across(): return lax.ppermute(array, 'blk', [(i, i ^ offset) for i in range(devices)])]
    ppermute x4 -> x3, waiting for transfers between devices: 3.41 us -> 0.45 us  [across_both(): return lax.ppermute(array, ('blk', 'head'), route)]
    pallas_call x3 -> x5, Pallas kernels: 10.4 us -> 13.3 us  [tile_grads(): pl.pallas_call(functools.partial(tile_kernel, shape), out_shape=out_shape...]
    squeeze x0 -> x1, local copies, waits for them, and re-layouts: none -> 0.72 us  [on_device(): own_k, own_v = (own[0], own[1])]
    add x1, other arithmetic: 0.75 us -> 0.04 us  [on_device(): own = own + across(both.astype(low), offset).astype(wide)]
    ppermute x14 -> x13, waiting for transfers between devices: 11.1 us -> 10.5 us  [across(): return lax.ppermute(array, 'blk', [(i, i ^ offset) for i in range(devices)])]
  transfers between devices with their start and end apart: 18 -> 16, of which waited for: 7 -> 6; matrix products, arithmetic and copies ran while one was open for 2% -> 2% of each run, Pallas kernels for 14% -> 20%
where the time goes in v2:
time: 49.2 us; the launch traced here: 49.1 us
  starting transfers between devices  21.1 us (43%)
  Pallas kernels  14.8 us (30%)
  waiting for transfers between devices  10.9 us (22%)
  other arithmetic  0.83 us (2%)
  between operations  0.74 us (2%)
  local copies, waits for them, and re-layouts  0.72 us (1%)
    ppermute x13, starting transfers between devices, across(): return lax.ppermute(array, 'blk', [(i, i ^ offset) for i in range(devices)])  18.1 us
    pallas_call x5, Pallas kernels, tile_grads(): pl.pallas_call(functools.partial(tile_kernel, shape), out_shape=out_shape...  13.3 us
    ppermute x13, waiting for transfers between devices, across(): return lax.ppermute(array, 'blk', [(i, i ^ offset) for i in range(devices)])  10.5 us
    ppermute x3, starting transfers between devices, across_both(): return lax.ppermute(array, ('blk', 'head'), route)  2.96 us
    pallas_call x1, Pallas kernels, pack(): pl.pallas_call(functools.partial(pack_kernel, split), out_shape=[jax.Shap...  1.42 us
  transfers between devices with their start and end apart: 16, of which 6 were waited for; matrix products, arithmetic and copies ran while one was open for 2% of the time, Pallas kernels for 20%

profile of v2, /device:TPU:0, one launch (start us, length us, event | category | flops | bytes accessed | tf_op | source)
XLA Modules:
  0.0 49.1 jit_solution(4357530052973971513)
XLA Ops:
  0.6 1.4 %pack.1 = (bf16[1056,128]{1,0:T(8,128)(2,1)S(1)}, bf16[2,256,128]{2,1,0:T(8,128)(2,1)S(1)}, bf16[4,256,128]{2,1,0:T(8,128)(2,1)S(1)}) custom-call(bf16[512,128]{1,0:T(8,128)(2,1)} %refs_0_.6, bf16[512,128]{1,0:T(8,128)(2,1)} %refs_1_.1, bf16[512,128]{1,0:T(8,128)(2,1)} %bitcast.9, bf16[512,128]{1,0:T(8,128)(2,1)} %bitcast.10, bf16[512,128]{1,0:T(8,128)(2,1)} %bitcast.11, ...), custom_call_target="tpu_custom_call" | custom-call | tf_op jit(solution)/shard_map/pack/pallas_call | solution.py:70
  2.1 4.1 %collective-permute-start.3 = (bf16[2,256,128]{2,1,0:T(8,128)(2,1)S(1)}, bf16[2,256,128]{2,1,0:T(8,128)(2,1)S(1)}, u32[]{:S(2)}, u32[]{:S(2)}) collective-permute-start(bf16[2,256,128]{2,1,0:T(8,128)(2,1)S(1)} %get-tuple-element.28), channel_id=1, source_target_pairs={{0,16},{2,18},{4,20},{6,22},{8,24},{10,26},{12,28},{14,30},{16,0},... | collective-permute-start | bytes 393224 | tf_op jit(solution)/shard_map/ppermute | solution.py:313
  6.2 1.5 %collective-permute-start = (bf16[1056,128]{1,0:T(8,128)(2,1)S(1)}, bf16[1056,128]{1,0:T(8,128)(2,1)S(1)}, u32[]{:S(2)}, u32[]{:S(2)}) collective-permute-start(bf16[1056,128]{1,0:T(8,128)(2,1)S(1)} %get-tuple-element.27.refs_1_), channel_id=1, source_target_pairs={{0,4},{2,6},{4,0},{6,2},{8,12},{10,14},{12,8},{14,10},{16,20},{18,... | collective-permute-start | bytes 811016 | tf_op jit(solution)/shard_map/ppermute | solution.py:313
  7.7 4.8 %collective-permute-done.3.refs_3_.refs_5_ = bf16[2,256,128]{2,1,0:T(8,128)(2,1)S(1)} collective-permute-done((bf16[2,256,128]{2,1,0:T(8,128)(2,1)S(1)}, bf16[2,256,128]{2,1,0:T(8,128)(2,1)S(1)}, u32[]{:S(2)}, u32[]{:S(2)}) %collective-permute-start.3) | collective-permute-done | bytes 131104 | tf_op jit(solution)/shard_map/ppermute | solution.py:313
  12.5 1.6 %collective-permute-start.4 = (bf16[2,256,128]{2,1,0:T(8,128)(2,1)S(1)}, bf16[2,256,128]{2,1,0:T(8,128)(2,1)S(1)}, u32[]{:S(2)}, u32[]{:S(2)}) collective-permute-start(bf16[2,256,128]{2,1,0:T(8,128)(2,1)S(1)} %collective-permute-done.3.refs_3_.refs_5_), channel_id=1, source_target_pairs={{0,1},{1,0},{2,3},{3,2},{4,5},{5,4},{6,7},{7,6},{8,9},{9,8},{10,11... | collective-permute-start | bytes 393224 | tf_op jit(solution)/shard_map/ppermute | solution.py:317
  14.1 0.7 %collective-permute-start.1 = (bf16[1056,128]{1,0:T(8,128)(2,1)S(1)}, bf16[1056,128]{1,0:T(8,128)(2,1)S(1)}, u32[]{:S(2)}, u32[]{:S(2)}) collective-permute-start(bf16[1056,128]{1,0:T(8,128)(2,1)S(1)} %get-tuple-element.27.refs_1_), channel_id=1, source_target_pairs={{0,8},{2,10},{4,12},{6,14},{8,0},{10,2},{12,4},{14,6},{16,24},{18,... | collective-permute-start | bytes 811016 | tf_op jit(solution)/shard_map/ppermute | solution.py:313
  14.7 2.3 %collective-permute-start.2 = (bf16[1056,128]{1,0:T(8,128)(2,1)S(1)}, bf16[1056,128]{1,0:T(8,128)(2,1)S(1)}, u32[]{:S(2)}, u32[]{:S(2)}) collective-permute-start(bf16[1056,128]{1,0:T(8,128)(2,1)S(1)} %get-tuple-element.27.refs_1_), channel_id=1, source_target_pairs={{0,12},{2,14},{4,8},{6,10},{8,4},{10,6},{12,0},{14,2},{16,28},{18,... | collective-permute-start | bytes 811016 | tf_op jit(solution)/shard_map/ppermute | solution.py:313
  17.5 0.5 %collective-permute-start.6 = (bf16[2,256,128]{2,1,0:T(8,128)(2,1)S(1)}, bf16[2,256,128]{2,1,0:T(8,128)(2,1)S(1)}, u32[]{:S(2)}, u32[]{:S(2)}) collective-permute-start(bf16[2,256,128]{2,1,0:T(8,128)(2,1)S(1)} %collective-permute-done.4.refs_6_), channel_id=1, source_target_pairs={{0,2},{2,0},{4,6},{6,4},{8,10},{10,8},{12,14},{14,12},{16,18},{18,... | collective-permute-start | bytes 393224 | tf_op jit(solution)/shard_map/ppermute | solution.py:313
  18.0 2.5 %tile_grads.5 = (f32[2,128,256]{2,1,0:T(8,128)S(1)}, f32[8,256,128]{2,1,0:T(8,128)S(1)}) custom-call(s32[32]{0:T(128)S(1)} %copy-done, bf16[1056,128]{1,0:T(8,128)(2,1)S(1)} %get-tuple-element.27.refs_1_, bf16[4,256,128]{2,1,0:T(8,128)(2,1)S(1)} %get-tuple-element.29.refs_2_.refs_3_, bf16[4,256,128]{2,1,0:T(8,128)(2,1)S(1)} %collective-permute-done.7.refs_3_.refs_4_), custom_call_target="tpu_custom_call" | custom-call | flops 335544320 | bytes 1572864 | tf_op jit(solution)/shard_map/tile_grads/pallas_call | solution.py:235
  20.5 1.6 %tile_grads.6 = (f32[2,128,256]{2,1,0:T(8,128)S(1)}, f32[2,128,256]{2,1,0:T(8,128)S(1)}, f32[4,256,128]{2,1,0:T(8,128)S(1)}) custom-call(s32[32]{0:T(128)S(1)} %copy-done, bf16[1056,128]{1,0:T(8,128)(2,1)S(1)} %get-tuple-element.27.refs_1_, bf16[1056,128]{1,0:T(8,128)(2,1)S(1)} %collective-permute-done.refs_2_.refs_1_, ...), custom_call_target="tpu_custom_call" | custom-call | flops 335544320 | bytes 1572864 | tf_op jit(solution)/shard_map/tile_grads/pallas_call | solution.py:235
  22.1 1.4 %collective-permute-done.1.refs_2_.refs_3_ = bf16[1056,128]{1,0:T(8,128)(2,1)S(1)} collective-permute-done((bf16[1056,128]{1,0:T(8,128)(2,1)S(1)}, bf16[1056,128]{1,0:T(8,128)(2,1)S(1)}, u32[]{:S(2)}, u32[]{:S(2)}) %collective-permute-start.1) | collective-permute-done | bytes 270368 | tf_op jit(solution)/shard_map/ppermute | solution.py:313
  23.4 3.3 %tile_grads.7 = (f32[2,128,256]{2,1,0:T(8,128)S(1)}, f32[2,128,256]{2,1,0:T(8,128)S(1)}, f32[8,256,128]{2,1,0:T(8,128)S(1)}) custom-call(s32[32]{0:T(128)S(1)} %copy-done, bf16[1056,128]{1,0:T(8,128)(2,1)S(1)} %collective-permute-done.refs_2_.refs_1_, bf16[1056,128]{1,0:T(8,128)(2,1)S(1)} %collective-permute-done.1.refs_2_.refs_3_, ...), custom_call_target="tpu_custom_call" | custom-call | flops 671088640 | bytes 2097152 | tf_op jit(solution)/shard_map/tile_grads/pallas_call | solution.py:235
  26.7 1.2 %collective-permute-done.2.refs_4_.refs_1_ = bf16[1056,128]{1,0:T(8,128)(2,1)S(1)} collective-permute-done((bf16[1056,128]{1,0:T(8,128)(2,1)S(1)}, bf16[1056,128]{1,0:T(8,128)(2,1)S(1)}, u32[]{:S(2)}, u32[]{:S(2)}) %collective-permute-start.2) | collective-permute-done | bytes 270368 | tf_op jit(solution)/shard_map/ppermute | solution.py:313
  27.9 3.4 %tile_grads.8 = (f32[512,128]{1,0:T(8,128)S(1)}, bf16[512,128]{1,0:T(8,128)(2,1)S(1)}, bf16[512,128]{1,0:T(8,128)(2,1)S(1)}, f32[2,128,256]{2,1,0:T(8,128)S(1)},...) custom-call(s32[32]{0:T(128)S(1)} %copy-done, bf16[1056,128]{1,0:T(8,128)(2,1)S(1)} %get-tuple-element.27.refs_1_, ...), custom_call_target="tpu_custom_call" | custom-call | flops 1342177280 | bytes 3145728 | tf_op jit(solution)/shard_map/tile_grads/pallas_call | solution.py:235
  31.4 2.5 %tile_grads.9 = (bf16[512,128]{1,0:T(8,128)(2,1)S(1)}, bf16[4,256,128]{2,1,0:T(8,128)(2,1)S(1)}, f32[4,256,128]{2,1,0:T(8,128)S(1)}) custom-call(s32[32]{0:T(128)S(1)} %copy-done, bf16[1056,128]{1,0:T(8,128)(2,1)S(1)} %collective-permute-done.2.refs_4_.refs_1_, bf16[4,256,128]{2,1,0:T(8,128)(2,1)S(1)} %get-tuple-element.29.refs_2_.refs_3_, ...), custom_call_target="tpu_custom_call" | custom-call | flops 335544320 | bytes 1572864 | tf_op jit(solution)/shard_map/tile_grads/pallas_call | solution.py:235
  33.9 0.6 %collective-permute-start.11 = (bf16[4,256,128]{2,1,0:T(8,128)(2,1)S(1)}, bf16[4,256,128]{2,1,0:T(8,128)(2,1)S(1)}, u32[]{:S(2)}, u32[]{:S(2)}) collective-permute-start(bf16[4,256,128]{2,1,0:T(8,128)(2,1)S(1)} %get-tuple-element.44), channel_id=1, source_target_pairs={{0,2},{2,0},{4,6},{6,4},{8,10},{10,8},{12,14},{14,12},{16,18},{18,... | collective-permute-start | bytes 786440 | tf_op jit(solution)/shard_map/ppermute | solution.py:313
  34.6 2.8 %collective-permute-start.8 = (bf16[512,128]{1,0:T(8,128)(2,1)S(1)}, bf16[512,128]{1,0:T(8,128)(2,1)S(1)}, u32[]{:S(2)}, u32[]{:S(2)}) collective-permute-start(bf16[512,128]{1,0:T(8,128)(2,1)S(1)} %get-tuple-element.38), channel_id=1, source_target_pairs={{0,4},{2,6},{4,0},{6,2},{8,12},{10,14},{12,8},{14,10},{16,20},{18,... | collective-permute-start | bytes 393224 | tf_op jit(solution)/shard_map/ppermute | solution.py:313
  37.4 1.5 %collective-permute-start.10 = (bf16[512,128]{1,0:T(8,128)(2,1)S(1)}, bf16[512,128]{1,0:T(8,128)(2,1)S(1)}, u32[]{:S(2)}, u32[]{:S(2)}) collective-permute-start(bf16[512,128]{1,0:T(8,128)(2,1)S(1)} %get-tuple-element.42), channel_id=1, source_target_pairs={{0,12},{2,14},{4,8},{6,10},{8,4},{10,6},{12,0},{14,2},{16,28},{18,... | collective-permute-start | bytes 393224 | tf_op jit(solution)/shard_map/ppermute | solution.py:313
  38.9 1.3 %collective-permute-start.12 = (bf16[2,256,128]{2,1,0:T(8,128)(2,1)S(1)}, bf16[2,256,128]{2,1,0:T(8,128)(2,1)S(1)}, u32[]{:S(2)}, u32[]{:S(2)}) collective-permute-start(bf16[2,256,128]{2,1,0:T(8,128)(2,1)S(1)} %get-tuple-element.46), channel_id=1, source_target_pairs={{0,1},{1,0},{2,3},{3,2},{4,5},{5,4},{6,7},{7,6},{8,9},{9,8},{10,11... | collective-permute-start | bytes 393224 | tf_op jit(solution)/shard_map/ppermute | solution.py:317
  40.3 4.2 %collective-permute-start.15 = (bf16[2,256,128]{2,1,0:T(8,128)(2,1)S(1)}, bf16[2,256,128]{2,1,0:T(8,128)(2,1)S(1)}, u32[]{:S(2)}, u32[]{:S(2)}) collective-permute-start(bf16[2,256,128]{2,1,0:T(8,128)(2,1)S(1)} %add_convert_fusion), channel_id=1, source_target_pairs={{0,16},{2,18},{4,20},{6,22},{8,24},{10,26},{12,28},{14,30},{16,0},... | collective-permute-start | bytes 393224 | tf_op jit(solution)/shard_map/ppermute | solution.py:313
  44.4 2.2 %collective-permute-done.10 = bf16[512,128]{1,0:T(8,128)(2,1)S(1)} collective-permute-done((bf16[512,128]{1,0:T(8,128)(2,1)S(1)}, bf16[512,128]{1,0:T(8,128)(2,1)S(1)}, u32[]{:S(2)}, u32[]{:S(2)}) %collective-permute-start.10) | collective-permute-done | bytes 131104 | tf_op jit(solution)/shard_map/ppermute | solution.py:313
  46.6 0.8 %add_bitcast_fusion = f32[1,512,128]{2,1,0:T(8,128)} fusion(bf16[512,128]{1,0:T(8,128)(2,1)S(1)} %collective-permute-done.10, bf16[512,128]{1,0:T(8,128)(2,1)S(1)} %collective-permute-done.9, f32[512,128]{1,0:T(8,128)S(1)} %get-tuple-element.37, bf16[512,128]{1,0:T(8,128)(2,1)S(1)} %collective-permute-done.8), kind=kLoop, calls=%fused_computation.2 | loop fusion | flops 393216 | bytes 917504 | tf_op jit(solution)/shard_map/broadcast_in_dim | solution.py:393
  47.4 0.9 %collective-permute-done.15 = bf16[2,256,128]{2,1,0:T(8,128)(2,1)S(1)} collective-permute-done((bf16[2,256,128]{2,1,0:T(8,128)(2,1)S(1)}, bf16[2,256,128]{2,1,0:T(8,128)(2,1)S(1)}, u32[]{:S(2)}, u32[]{:S(2)}) %collective-permute-start.15) | collective-permute-done | bytes 131104 | tf_op jit(solution)/shard_map/ppermute | solution.py:313
  48.4 0.7 %slice_bitcast_fusion = (f32[256,128]{1,0:T(8,128)}, f32[256,128]{1,0:T(8,128)}) fusion(f32[2,256,128]{2,1,0:T(8,128)S(1)} %convert_add_fusion), kind=kLoop, calls=%fused_computation.3 | loop fusion | bytes 524288 | tf_op jit(solution)/shard_map/squeeze | solution.py:378
  (22 shorter events, 0.8 us)
Async XLA Ops:
  2.1 10.4 %collective-permute-start.3 = (bf16[2,256,128]{2,1,0:T(8,128)(2,1)S(1)}, bf16[2,256,128]{2,1,0:T(8,128)(2,1)S(1)}, u32[]{:S(2)}, u32[]{:S(2)}) collective-permute-start(bf16[2,256,128]{2,1,0:T(8,128)(2,1)S(1)} %get-tuple-element.28), channel_id=1, source_target_pairs={{0,16},{2,18},{4,20},{6,22},{8,24},{10,26},{12,28},{14,30},{16,0},... | collective-permute-start | bytes 393224 | tf_op jit(solution)/shard_map/ppermute | solution.py:313
  6.2 11.8 %copy-start = (s32[32]{0:T(128)S(1)}, s32[32]{0:T(128)}, u32[]{:S(2)}) copy-start(s32[32]{0:T(128)} %refs_0_.11) | copy-start | bytes 388
  6.2 11.3 %collective-permute-start.7 = (bf16[4,256,128]{2,1,0:T(8,128)(2,1)S(1)}, bf16[4,256,128]{2,1,0:T(8,128)(2,1)S(1)}, u32[]{:S(2)}, u32[]{:S(2)}) collective-permute-start(bf16[4,256,128]{2,1,0:T(8,128)(2,1)S(1)} %get-tuple-element.29.refs_2_.refs_3_), channel_id=1, source_target_pairs={{0,2},{2,0},{4,6},{6,4},{8,10},{10,8},{12,14},{14,12},{16,18},{18,... | collective-permute-start | bytes 786440 | tf_op jit(solution)/shard_map/ppermute | solution.py:313
  6.2 14.3 %collective-permute-start = (bf16[1056,128]{1,0:T(8,128)(2,1)S(1)}, bf16[1056,128]{1,0:T(8,128)(2,1)S(1)}, u32[]{:S(2)}, u32[]{:S(2)}) collective-permute-start(bf16[1056,128]{1,0:T(8,128)(2,1)S(1)} %get-tuple-element.27.refs_1_), channel_id=1, source_target_pairs={{0,4},{2,6},{4,0},{6,2},{8,12},{10,14},{12,8},{14,10},{16,20},{18,... | collective-permute-start | bytes 811016 | tf_op jit(solution)/shard_map/ppermute | solution.py:313
  12.5 5.0 %collective-permute-start.4 = (bf16[2,256,128]{2,1,0:T(8,128)(2,1)S(1)}, bf16[2,256,128]{2,1,0:T(8,128)(2,1)S(1)}, u32[]{:S(2)}, u32[]{:S(2)}) collective-permute-start(bf16[2,256,128]{2,1,0:T(8,128)(2,1)S(1)} %collective-permute-done.3.refs_3_.refs_5_), channel_id=1, source_target_pairs={{0,1},{1,0},{2,3},{3,2},{4,5},{5,4},{6,7},{7,6},{8,9},{9,8},{10,11... | collective-permute-start | bytes 393224 | tf_op jit(solution)/shard_map/ppermute | solution.py:317
  14.1 9.4 %collective-permute-start.1 = (bf16[1056,128]{1,0:T(8,128)(2,1)S(1)}, bf16[1056,128]{1,0:T(8,128)(2,1)S(1)}, u32[]{:S(2)}, u32[]{:S(2)}) collective-permute-start(bf16[1056,128]{1,0:T(8,128)(2,1)S(1)} %get-tuple-element.27.refs_1_), channel_id=1, source_target_pairs={{0,8},{2,10},{4,12},{6,14},{8,0},{10,2},{12,4},{14,6},{16,24},{18,... | collective-permute-start | bytes 811016 | tf_op jit(solution)/shard_map/ppermute | solution.py:313
  14.7 13.2 %collective-permute-start.2 = (bf16[1056,128]{1,0:T(8,128)(2,1)S(1)}, bf16[1056,128]{1,0:T(8,128)(2,1)S(1)}, u32[]{:S(2)}, u32[]{:S(2)}) collective-permute-start(bf16[1056,128]{1,0:T(8,128)(2,1)S(1)} %get-tuple-element.27.refs_1_), channel_id=1, source_target_pairs={{0,12},{2,14},{4,8},{6,10},{8,4},{10,6},{12,0},{14,2},{16,28},{18,... | collective-permute-start | bytes 811016 | tf_op jit(solution)/shard_map/ppermute | solution.py:313
  17.5 3.0 %collective-permute-start.5 = (bf16[2,256,128]{2,1,0:T(8,128)(2,1)S(1)}, bf16[2,256,128]{2,1,0:T(8,128)(2,1)S(1)}, u32[]{:S(2)}, u32[]{:S(2)}) collective-permute-start(bf16[2,256,128]{2,1,0:T(8,128)(2,1)S(1)} %collective-permute-done.3.refs_3_.refs_5_), channel_id=1, source_target_pairs={{0,2},{2,0},{4,6},{6,4},{8,10},{10,8},{12,14},{14,12},{16,18},{18,... | collective-permute-start | bytes 393224 | tf_op jit(solution)/shard_map/ppermute | solution.py:313
  17.5 10.4 %collective-permute-start.6 = (bf16[2,256,128]{2,1,0:T(8,128)(2,1)S(1)}, bf16[2,256,128]{2,1,0:T(8,128)(2,1)S(1)}, u32[]{:S(2)}, u32[]{:S(2)}) collective-permute-start(bf16[2,256,128]{2,1,0:T(8,128)(2,1)S(1)} %collective-permute-done.4.refs_6_), channel_id=1, source_target_pairs={{0,2},{2,0},{4,6},{6,4},{8,10},{10,8},{12,14},{14,12},{16,18},{18,... | collective-permute-start | bytes 393224 | tf_op jit(solution)/shard_map/ppermute | solution.py:313
  31.3 3.1 %collective-permute-start.13 = (bf16[4,256,128]{2,1,0:T(8,128)(2,1)S(1)}, bf16[4,256,128]{2,1,0:T(8,128)(2,1)S(1)}, u32[]{:S(2)}, u32[]{:S(2)}) collective-permute-start(bf16[4,256,128]{2,1,0:T(8,128)(2,1)S(1)} %get-tuple-element.48), channel_id=1, source_target_pairs={{0,2},{2,0},{4,6},{6,4},{8,10},{10,8},{12,14},{14,12},{16,18},{18,... | collective-permute-start | bytes 786440 | tf_op jit(solution)/shard_map/ppermute | solution.py:313
  33.9 4.9 %collective-permute-start.11 = (bf16[4,256,128]{2,1,0:T(8,128)(2,1)S(1)}, bf16[4,256,128]{2,1,0:T(8,128)(2,1)S(1)}, u32[]{:S(2)}, u32[]{:S(2)}) collective-permute-start(bf16[4,256,128]{2,1,0:T(8,128)(2,1)S(1)} %get-tuple-element.44), channel_id=1, source_target_pairs={{0,2},{2,0},{4,6},{6,4},{8,10},{10,8},{12,14},{14,12},{16,18},{18,... | collective-permute-start | bytes 786440 | tf_op jit(solution)/shard_map/ppermute | solution.py:313
  34.5 5.7 %collective-permute-start.14 = (bf16[2,256,128]{2,1,0:T(8,128)(2,1)S(1)}, bf16[2,256,128]{2,1,0:T(8,128)(2,1)S(1)}, u32[]{:S(2)}, u32[]{:S(2)}) collective-permute-start(bf16[2,256,128]{2,1,0:T(8,128)(2,1)S(1)} %get-tuple-element.50), channel_id=1, source_target_pairs={{0,1},{1,0},{2,3},{3,2},{4,5},{5,4},{6,7},{7,6},{8,9},{9,8},{10,11... | collective-permute-start | bytes 393224 | tf_op jit(solution)/shard_map/ppermute | solution.py:317
  34.6 9.8 %collective-permute-start.8 = (bf16[512,128]{1,0:T(8,128)(2,1)S(1)}, bf16[512,128]{1,0:T(8,128)(2,1)S(1)}, u32[]{:S(2)}, u32[]{:S(2)}) collective-permute-start(bf16[512,128]{1,0:T(8,128)(2,1)S(1)} %get-tuple-element.38), channel_id=1, source_target_pairs={{0,4},{2,6},{4,0},{6,2},{8,12},{10,14},{12,8},{14,10},{16,20},{18,... | collective-permute-start | bytes 393224 | tf_op jit(solution)/shard_map/ppermute | solution.py:313
  37.4 7.1 %collective-permute-start.9 = (bf16[512,128]{1,0:T(8,128)(2,1)S(1)}, bf16[512,128]{1,0:T(8,128)(2,1)S(1)}, u32[]{:S(2)}, u32[]{:S(2)}) collective-permute-start(bf16[512,128]{1,0:T(8,128)(2,1)S(1)} %get-tuple-element.39), channel_id=1, source_target_pairs={{0,8},{2,10},{4,12},{6,14},{8,0},{10,2},{12,4},{14,6},{16,24},{18,... | collective-permute-start | bytes 393224 | tf_op jit(solution)/shard_map/ppermute | solution.py:313
  37.4 9.3 %collective-permute-start.10 = (bf16[512,128]{1,0:T(8,128)(2,1)S(1)}, bf16[512,128]{1,0:T(8,128)(2,1)S(1)}, u32[]{:S(2)}, u32[]{:S(2)}) collective-permute-start(bf16[512,128]{1,0:T(8,128)(2,1)S(1)} %get-tuple-element.42), channel_id=1, source_target_pairs={{0,12},{2,14},{4,8},{6,10},{8,4},{10,6},{12,0},{14,2},{16,28},{18,... | collective-permute-start | bytes 393224 | tf_op jit(solution)/shard_map/ppermute | solution.py:313
  38.9 8.5 %collective-permute-start.12 = (bf16[2,256,128]{2,1,0:T(8,128)(2,1)S(1)}, bf16[2,256,128]{2,1,0:T(8,128)(2,1)S(1)}, u32[]{:S(2)}, u32[]{:S(2)}) collective-permute-start(bf16[2,256,128]{2,1,0:T(8,128)(2,1)S(1)} %get-tuple-element.46), channel_id=1, source_target_pairs={{0,1},{1,0},{2,3},{3,2},{4,5},{5,4},{6,7},{7,6},{8,9},{9,8},{10,11... | collective-permute-start | bytes 393224 | tf_op jit(solution)/shard_map/ppermute | solution.py:317
  40.3 8.1 %collective-permute-start.15 = (bf16[2,256,128]{2,1,0:T(8,128)(2,1)S(1)}, bf16[2,256,128]{2,1,0:T(8,128)(2,1)S(1)}, u32[]{:S(2)}, u32[]{:S(2)}) collective-permute-start(bf16[2,256,128]{2,1,0:T(8,128)(2,1)S(1)} %add_convert_fusion), channel_id=1, source_target_pairs={{0,16},{2,18},{4,20},{6,22},{8,24},{10,26},{12,28},{14,30},{16,0},... | collective-permute-start | bytes 393224 | tf_op jit(solution)/shard_map/ppermute | solution.py:313

commit v3 on v2

--- a/solution.py
+++ b/solution.py
@@ -12,7 +12,6 @@
 WIDTH = 4
 LIMIT = 24 * 2**20
 VMEM = pl.BlockSpec(memory_space=pltpu.VMEM)
-SMEM = pl.BlockSpec(memory_space=pltpu.SMEM)
 
 
 def contract(left, right, dims):
@@ -104,6 +103,11 @@
     me = lax.axis_index("blk")
     head = lax.axis_index("head")
     lines = rows // width
+    lane = lax.broadcasted_iota(jnp.int32, order.shape, 1)
+
+    def place(block_index):
+        return jnp.sum(jnp.where(lane == block_index, order[...], 0.0)).astype(jnp.int32)
+
     for u, offset in enumerate(q_units):
         stats = q_in[u][2 * rows :].astype(jnp.float32)
         for half in range(2):
@@ -119,7 +123,7 @@
                 out[i] = jnp.concatenate(
                     [row[c : c + 1] for c in range(start, start + lines // 2)], axis=1
                 )
-            q_at[i] = order[2 * (me ^ offset) + half]
+            q_at[i] = place(2 * (me ^ offset) + half)
             if offset in q_before:
                 dqt[i] = q_before[offset][half]
             else:
@@ -130,7 +134,7 @@
         v[j] = ref[at + 1]
         kt[j] = ref[at].T
         half = lax.rem(head + part, 2) if split else part
-        k_at[j] = order[2 * (me ^ offset) + half]
+        k_at[j] = place(2 * (me ^ offset) + half)
         for t in range(2):
             if blocks[j] in k_held:
                 total[2 * j + t] = k_before[2 * k_held.index(blocks[j]) + t]
@@ -235,7 +239,7 @@
     outs = pl.pallas_call(
         functools.partial(tile_kernel, shape),
         out_shape=out_shape,
-        in_specs=[SMEM] + [VMEM] * len(operands),
+        in_specs=[VMEM] * (1 + len(operands)),
         out_specs=[VMEM] * len(out_shape),
         scratch_shapes=[
             pltpu.VMEM((n_q, block, width), jnp.bfloat16),
@@ -337,7 +341,8 @@
     home = [o for o in k_units if o < 2]
     away = [o for o in k_units if o >= 2]
     mine, near, late = q_units[:1], q_units[1:-1], q_units[-1:]
-    tile = functools.partial(tile_grads, block_order, split=split, rows=rows, scale=scale)
+    order = block_order.astype(jnp.float32)[None]
+    tile = functools.partial(tile_grads, order, split=split, rows=rows, scale=scale)
     home_kv, away_kv = some(held, home), some(held, away)
     home_blocks = blocks_of(home_kv)
     held_q, (total,) = tile(some(q, mine), home_kv, {}, None, (), False)

time: 49.2 us -> 52.2 us (1.061)
  waiting for transfers between devices: 10.9 us -> 17.2 us
  Pallas kernels: 14.8 us -> 12.3 us
  starting transfers between devices: 21.1 us -> 20.2 us
    ppermute x13, waiting for transfers between devices: 10.5 us -> 17.2 us  [across(): return lax.ppermute(array, 'blk', [(i, i ^ offset) for i in range(devices)])]
    pallas_call x5, Pallas kernels: 13.3 us -> 10.8 us  [tile_grads(): pl.pallas_call(functools.partial(tile_kernel, shape), out_shape=out_shape...]
    ppermute x3, starting transfers between devices: 2.96 us -> 2.37 us  [across_both(): return lax.ppermute(array, ('blk', 'head'), route)]
  transfers between devices with their start and end apart: 16 -> 16, of which waited for: 6 -> 5; matrix products, arithmetic and copies ran while one was open for 2% -> 2% of each run, Pallas kernels for 20% -> 15%
where the time goes in v3:
time: 52.2 us; the launch traced here: 52 us
  starting transfers between devices  20.2 us (39%)
  waiting for transfers between devices  17.2 us (33%)
  Pallas kernels  12.3 us (24%)
  other arithmetic  0.84 us (2%)
  between operations  0.76 us (1%)
  local copies, waits for them, and re-layouts  0.72 us (1%)
    ppermute x13, starting transfers between devices, across(): return lax.ppermute(array, 'blk', [(i, i ^ offset) for i in range(devices)])  17.8 us
    ppermute x13, waiting for transfers between devices, across(): return lax.ppermute(array, 'blk', [(i, i ^ offset) for i in range(devices)])  17.2 us
    pallas_call x5, Pallas kernels, tile_grads(): pl.pallas_call(functools.partial(tile_kernel, shape), out_shape=out_shape...  10.8 us
    ppermute x3, starting transfers between devices, across_both(): return lax.ppermute(array, ('blk', 'head'), route)  2.37 us
    pallas_call x1, Pallas kernels, pack(): pl.pallas_call(functools.partial(pack_kernel, split), out_shape=[jax.Shap...  1.42 us
  transfers between devices with their start and end apart: 16, of which 5 were waited for; matrix products, arithmetic and copies ran while one was open for 2% of the time, Pallas kernels for 15%

profile of v3, /device:TPU:0, one launch (start us, length us, event | category | flops | bytes accessed | tf_op | source)
XLA Modules:
  0.0 52.0 jit_solution(11118665505218250265)
XLA Ops:
  0.6 1.4 %pack.1 = (bf16[1056,128]{1,0:T(8,128)(2,1)S(1)}, bf16[2,256,128]{2,1,0:T(8,128)(2,1)S(1)}, bf16[4,256,128]{2,1,0:T(8,128)(2,1)S(1)}) custom-call(bf16[512,128]{1,0:T(8,128)(2,1)} %refs_0_.1, bf16[512,128]{1,0:T(8,128)(2,1)} %refs_1_.1, bf16[512,128]{1,0:T(8,128)(2,1)} %bitcast.11, bf16[512,128]{1,0:T(8,128)(2,1)} %bitcast.12, bf16[512,128]{1,0:T(8,128)(2,1)} %bitcast.13, ...), custom_call_target="tpu_custom_call" | custom-call | tf_op jit(solution)/shard_map/pack/pallas_call | solution.py:69
  2.1 4.1 %collective-permute-start.3 = (bf16[2,256,128]{2,1,0:T(8,128)(2,1)S(1)}, bf16[2,256,128]{2,1,0:T(8,128)(2,1)S(1)}, u32[]{:S(2)}, u32[]{:S(2)}) collective-permute-start(bf16[2,256,128]{2,1,0:T(8,128)(2,1)S(1)} %get-tuple-element.28), channel_id=1, source_target_pairs={{0,16},{2,18},{4,20},{6,22},{8,24},{10,26},{12,28},{14,30},{16,0},... | collective-permute-start | bytes 393224 | tf_op jit(solution)/shard_map/ppermute | solution.py:317
  6.2 6.3 %collective-permute-done.3.refs_3_.refs_5_ = bf16[2,256,128]{2,1,0:T(8,128)(2,1)S(1)} collective-permute-done((bf16[2,256,128]{2,1,0:T(8,128)(2,1)S(1)}, bf16[2,256,128]{2,1,0:T(8,128)(2,1)S(1)}, u32[]{:S(2)}, u32[]{:S(2)}) %collective-permute-start.3) | collective-permute-done | bytes 131104 | tf_op jit(solution)/shard_map/ppermute | solution.py:317
  12.5 1.6 %collective-permute-start.4 = (bf16[2,256,128]{2,1,0:T(8,128)(2,1)S(1)}, bf16[2,256,128]{2,1,0:T(8,128)(2,1)S(1)}, u32[]{:S(2)}, u32[]{:S(2)}) collective-permute-start(bf16[2,256,128]{2,1,0:T(8,128)(2,1)S(1)} %collective-permute-done.3.refs_3_.refs_5_), channel_id=1, source_target_pairs={{0,1},{1,0},{2,3},{3,2},{4,5},{5,4},{6,7},{7,6},{8,9},{9,8},{10,11... | collective-permute-start | bytes 393224 | tf_op jit(solution)/shard_map/ppermute | solution.py:321
  14.1 1.5 %collective-permute-start = (bf16[1056,128]{1,0:T(8,128)(2,1)S(1)}, bf16[1056,128]{1,0:T(8,128)(2,1)S(1)}, u32[]{:S(2)}, u32[]{:S(2)}) collective-permute-start(bf16[1056,128]{1,0:T(8,128)(2,1)S(1)} %get-tuple-element.27.refs_1_), channel_id=1, source_target_pairs={{0,4},{2,6},{4,0},{6,2},{8,12},{10,14},{12,8},{14,10},{16,20},{18,... | collective-permute-start | bytes 811016 | tf_op jit(solution)/shard_map/ppermute | solution.py:317
  15.6 0.6 %collective-permute-start.2 = (bf16[1056,128]{1,0:T(8,128)(2,1)S(1)}, bf16[1056,128]{1,0:T(8,128)(2,1)S(1)}, u32[]{:S(2)}, u32[]{:S(2)}) collective-permute-start(bf16[1056,128]{1,0:T(8,128)(2,1)S(1)} %get-tuple-element.27.refs_1_), channel_id=1, source_target_pairs={{0,12},{2,14},{4,8},{6,10},{8,4},{10,6},{12,0},{14,2},{16,28},{18,... | collective-permute-start | bytes 811016 | tf_op jit(solution)/shard_map/ppermute | solution.py:317
  16.2 1.4 %collective-permute-start.1 = (bf16[1056,128]{1,0:T(8,128)(2,1)S(1)}, bf16[1056,128]{1,0:T(8,128)(2,1)S(1)}, u32[]{:S(2)}, u32[]{:S(2)}) collective-permute-start(bf16[1056,128]{1,0:T(8,128)(2,1)S(1)} %get-tuple-element.27.refs_1_), channel_id=1, source_target_pairs={{0,8},{2,10},{4,12},{6,14},{8,0},{10,2},{12,4},{14,6},{16,24},{18,... | collective-permute-start | bytes 811016 | tf_op jit(solution)/shard_map/ppermute | solution.py:317
  17.6 0.5 collective-permute-start.6
  18.1 2.0 %tile_grads.5 = (f32[2,128,256]{2,1,0:T(8,128)S(1)}, f32[8,256,128]{2,1,0:T(8,128)S(1)}) custom-call(f32[1,32]{1,0:T(1,128)S(1)} %convert_bitcast_fusion.refs_0_, bf16[1056,128]{1,0:T(8,128)(2,1)S(1)} %get-tuple-element.27.refs_1_, bf16[4,256,128]{2,1,0:T(8,128)(2,1)S(1)} %get-tuple-element.29.refs_2_.refs_3_, ...), custom_call_target="tpu_custom_call" | custom-call | flops 335544320 | bytes 1572864 | tf_op jit(solution)/shard_map/tile_grads/pallas_call | solution.py:239
  20.1 6.9 %collective-permute-done.refs_2_.refs_1_ = bf16[1056,128]{1,0:T(8,128)(2,1)S(1)} collective-permute-done((bf16[1056,128]{1,0:T(8,128)(2,1)S(1)}, bf16[1056,128]{1,0:T(8,128)(2,1)S(1)}, u32[]{:S(2)}, u32[]{:S(2)}) %collective-permute-start) | collective-permute-done | bytes 270368 | tf_op jit(solution)/shard_map/ppermute | solution.py:317
  27.0 1.1 %tile_grads.6 = (f32[2,128,256]{2,1,0:T(8,128)S(1)}, f32[2,128,256]{2,1,0:T(8,128)S(1)}, f32[4,256,128]{2,1,0:T(8,128)S(1)}) custom-call(f32[1,32]{1,0:T(1,128)S(1)} %convert_bitcast_fusion.refs_0_, bf16[1056,128]{1,0:T(8,128)(2,1)S(1)} %get-tuple-element.27.refs_1_, bf16[1056,128]{1,0:T(8,128)(2,1)S(1)} %collective-permute-done.refs_2_.refs_1_, ...), custom_call_target="tpu_custom_call" | custom-call | flops 335544320 | bytes 1572864 | tf_op jit(solution)/shard_map/tile_grads/pallas_call | solution.py:239
  28.1 0.1 collective-permute-done.1.refs_2_.refs_3_
  28.2 2.8 %tile_grads.7 = (f32[2,128,256]{2,1,0:T(8,128)S(1)}, f32[2,128,256]{2,1,0:T(8,128)S(1)}, f32[8,256,128]{2,1,0:T(8,128)S(1)}) custom-call(f32[1,32]{1,0:T(1,128)S(1)} %convert_bitcast_fusion.refs_0_, bf16[1056,128]{1,0:T(8,128)(2,1)S(1)} %collective-permute-done.refs_2_.refs_1_, bf16[1056,128]{1,0:T(8,128)(2,1)S(1)} %collective-permute-done.1.refs_2_.refs_3_, ...), custom_call_target="tpu_custom_call" | custom-call | flops 671088640 | bytes 2097152 | tf_op jit(solution)/shard_map/tile_grads/pallas_call | solution.py:239
  31.0 3.0 %tile_grads.8 = (f32[512,128]{1,0:T(8,128)S(1)}, bf16[512,128]{1,0:T(8,128)(2,1)S(1)}, bf16[512,128]{1,0:T(8,128)(2,1)S(1)}, f32[2,128,256]{2,1,0:T(8,128)S(1)},...) custom-call(f32[1,32]{1,0:T(1,128)S(1)} %convert_bitcast_fusion.refs_0_, ...), custom_call_target="tpu_custom_call" | custom-call | flops 1342177280 | bytes 3145728 | tf_op jit(solution)/shard_map/tile_grads/pallas_call | solution.py:239
  34.1 2.0 %tile_grads.9 = (bf16[512,128]{1,0:T(8,128)(2,1)S(1)}, bf16[4,256,128]{2,1,0:T(8,128)(2,1)S(1)}, f32[4,256,128]{2,1,0:T(8,128)S(1)}) custom-call(f32[1,32]{1,0:T(1,128)S(1)} %convert_bitcast_fusion.refs_0_, bf16[1056,128]{1,0:T(8,128)(2,1)S(1)} %collective-permute-done.2.refs_4_.refs_1_, bf16[4,256,128]{2,1,0:T(8,128)(2,1)S(1)} %get-tuple-element.29.refs_2_.refs_3_, ...), custom_call_target="tpu_custom_call" | custom-call | flops 335544320 | bytes 1572864 | tf_op jit(solution)/shard_map/tile_grads/pallas_call | solution.py:239
  36.1 0.6 %collective-permute-start.11 = (bf16[4,256,128]{2,1,0:T(8,128)(2,1)S(1)}, bf16[4,256,128]{2,1,0:T(8,128)(2,1)S(1)}, u32[]{:S(2)}, u32[]{:S(2)}) collective-permute-start(bf16[4,256,128]{2,1,0:T(8,128)(2,1)S(1)} %get-tuple-element.44), channel_id=1, source_target_pairs={{0,2},{2,0},{4,6},{6,4},{8,10},{10,8},{12,14},{14,12},{16,18},{18,... | collective-permute-start | bytes 786440 | tf_op jit(solution)/shard_map/ppermute | solution.py:317
  36.8 3.9 %collective-permute-start.8 = (bf16[512,128]{1,0:T(8,128)(2,1)S(1)}, bf16[512,128]{1,0:T(8,128)(2,1)S(1)}, u32[]{:S(2)}, u32[]{:S(2)}) collective-permute-start(bf16[512,128]{1,0:T(8,128)(2,1)S(1)} %get-tuple-element.38), channel_id=1, source_target_pairs={{0,4},{2,6},{4,0},{6,2},{8,12},{10,14},{12,8},{14,10},{16,20},{18,... | collective-permute-start | bytes 393224 | tf_op jit(solution)/shard_map/ppermute | solution.py:317
  40.7 1.5 %collective-permute-start.10 = (bf16[512,128]{1,0:T(8,128)(2,1)S(1)}, bf16[512,128]{1,0:T(8,128)(2,1)S(1)}, u32[]{:S(2)}, u32[]{:S(2)}) collective-permute-start(bf16[512,128]{1,0:T(8,128)(2,1)S(1)} %get-tuple-element.42), channel_id=1, source_target_pairs={{0,12},{2,14},{4,8},{6,10},{8,4},{10,6},{12,0},{14,2},{16,28},{18,... | collective-permute-start | bytes 393224 | tf_op jit(solution)/shard_map/ppermute | solution.py:317
  42.2 0.7 %collective-permute-start.12 = (bf16[2,256,128]{2,1,0:T(8,128)(2,1)S(1)}, bf16[2,256,128]{2,1,0:T(8,128)(2,1)S(1)}, u32[]{:S(2)}, u32[]{:S(2)}) collective-permute-start(bf16[2,256,128]{2,1,0:T(8,128)(2,1)S(1)} %get-tuple-element.46), channel_id=1, source_target_pairs={{0,1},{1,0},{2,3},{3,2},{4,5},{5,4},{6,7},{7,6},{8,9},{9,8},{10,11... | collective-permute-start | bytes 393224 | tf_op jit(solution)/shard_map/ppermute | solution.py:321
  43.0 3.7 %collective-permute-start.15 = (bf16[2,256,128]{2,1,0:T(8,128)(2,1)S(1)}, bf16[2,256,128]{2,1,0:T(8,128)(2,1)S(1)}, u32[]{:S(2)}, u32[]{:S(2)}) collective-permute-start(bf16[2,256,128]{2,1,0:T(8,128)(2,1)S(1)} %add_convert_fusion), channel_id=1, source_target_pairs={{0,16},{2,18},{4,20},{6,22},{8,24},{10,26},{12,28},{14,30},{16,0},... | collective-permute-start | bytes 393224 | tf_op jit(solution)/shard_map/ppermute | solution.py:317
  46.6 2.5 %collective-permute-done.9 = bf16[512,128]{1,0:T(8,128)(2,1)S(1)} collective-permute-done((bf16[512,128]{1,0:T(8,128)(2,1)S(1)}, bf16[512,128]{1,0:T(8,128)(2,1)S(1)}, u32[]{:S(2)}, u32[]{:S(2)}) %collective-permute-start.9) | collective-permute-done | bytes 131104 | tf_op jit(solution)/shard_map/ppermute | solution.py:317
  49.2 1.3 %collective-permute-done.10 = bf16[512,128]{1,0:T(8,128)(2,1)S(1)} collective-permute-done((bf16[512,128]{1,0:T(8,128)(2,1)S(1)}, bf16[512,128]{1,0:T(8,128)(2,1)S(1)}, u32[]{:S(2)}, u32[]{:S(2)}) %collective-permute-start.10) | collective-permute-done | bytes 131104 | tf_op jit(solution)/shard_map/ppermute | solution.py:317
  50.5 0.8 %add_bitcast_fusion = f32[1,512,128]{2,1,0:T(8,128)} fusion(bf16[512,128]{1,0:T(8,128)(2,1)S(1)} %collective-permute-done.10, bf16[512,128]{1,0:T(8,128)(2,1)S(1)} %collective-permute-done.9, f32[512,128]{1,0:T(8,128)S(1)} %get-tuple-element.37, bf16[512,128]{1,0:T(8,128)(2,1)S(1)} %collective-permute-done.8), kind=kLoop, calls=%fused_computation.2 | loop fusion | flops 393216 | bytes 917504 | tf_op jit(solution)/shard_map/broadcast_in_dim | solution.py:398
  51.3 0.7 %slice_bitcast_fusion = (f32[256,128]{1,0:T(8,128)}, f32[256,128]{1,0:T(8,128)}) fusion(f32[2,256,128]{2,1,0:T(8,128)S(1)} %convert_add_fusion), kind=kLoop, calls=%fused_computation.3 | loop fusion | bytes 524288 | tf_op jit(solution)/shard_map/squeeze | solution.py:383
  (23 shorter events, 0.4 us)
Async XLA Ops:
  2.1 10.4 %collective-permute-start.3 = (bf16[2,256,128]{2,1,0:T(8,128)(2,1)S(1)}, bf16[2,256,128]{2,1,0:T(8,128)(2,1)S(1)}, u32[]{:S(2)}, u32[]{:S(2)}) collective-permute-start(bf16[2,256,128]{2,1,0:T(8,128)(2,1)S(1)} %get-tuple-element.28), channel_id=1, source_target_pairs={{0,16},{2,18},{4,20},{6,22},{8,24},{10,26},{12,28},{14,30},{16,0},... | collective-permute-start | bytes 393224 | tf_op jit(solution)/shard_map/ppermute | solution.py:317
  6.2 11.9 %copy-start = (s32[32]{0:T(128)S(1)}, s32[32]{0:T(128)}, u32[]{:S(2)}) copy-start(s32[32]{0:T(128)} %param.13) | copy-start | bytes 388
  6.2 11.4 %collective-permute-start.7 = (bf16[4,256,128]{2,1,0:T(8,128)(2,1)S(1)}, bf16[4,256,128]{2,1,0:T(8,128)(2,1)S(1)}, u32[]{:S(2)}, u32[]{:S(2)}) collective-permute-start(bf16[4,256,128]{2,1,0:T(8,128)(2,1)S(1)} %get-tuple-element.29.refs_2_.refs_3_), channel_id=1, source_target_pairs={{0,2},{2,0},{4,6},{6,4},{8,10},{10,8},{12,14},{14,12},{16,18},{18,... | collective-permute-start | bytes 786440 | tf_op jit(solution)/shard_map/ppermute | solution.py:317
  12.5 5.1 %collective-permute-start.4 = (bf16[2,256,128]{2,1,0:T(8,128)(2,1)S(1)}, bf16[2,256,128]{2,1,0:T(8,128)(2,1)S(1)}, u32[]{:S(2)}, u32[]{:S(2)}) collective-permute-start(bf16[2,256,128]{2,1,0:T(8,128)(2,1)S(1)} %collective-permute-done.3.refs_3_.refs_5_), channel_id=1, source_target_pairs={{0,1},{1,0},{2,3},{3,2},{4,5},{5,4},{6,7},{7,6},{8,9},{9,8},{10,11... | collective-permute-start | bytes 393224 | tf_op jit(solution)/shard_map/ppermute | solution.py:321
  14.1 12.9 %collective-permute-start = (bf16[1056,128]{1,0:T(8,128)(2,1)S(1)}, bf16[1056,128]{1,0:T(8,128)(2,1)S(1)}, u32[]{:S(2)}, u32[]{:S(2)}) collective-permute-start(bf16[1056,128]{1,0:T(8,128)(2,1)S(1)} %get-tuple-element.27.refs_1_), channel_id=1, source_target_pairs={{0,4},{2,6},{4,0},{6,2},{8,12},{10,14},{12,8},{14,10},{16,20},{18,... | collective-permute-start | bytes 811016 | tf_op jit(solution)/shard_map/ppermute | solution.py:317
  15.6 15.5 %collective-permute-start.2 = (bf16[1056,128]{1,0:T(8,128)(2,1)S(1)}, bf16[1056,128]{1,0:T(8,128)(2,1)S(1)}, u32[]{:S(2)}, u32[]{:S(2)}) collective-permute-start(bf16[1056,128]{1,0:T(8,128)(2,1)S(1)} %get-tuple-element.27.refs_1_), channel_id=1, source_target_pairs={{0,12},{2,14},{4,8},{6,10},{8,4},{10,6},{12,0},{14,2},{16,28},{18,... | collective-permute-start | bytes 811016 | tf_op jit(solution)/shard_map/ppermute | solution.py:317
  16.2 12.0 %collective-permute-start.1 = (bf16[1056,128]{1,0:T(8,128)(2,1)S(1)}, bf16[1056,128]{1,0:T(8,128)(2,1)S(1)}, u32[]{:S(2)}, u32[]{:S(2)}) collective-permute-start(bf16[1056,128]{1,0:T(8,128)(2,1)S(1)} %get-tuple-element.27.refs_1_), channel_id=1, source_target_pairs={{0,8},{2,10},{4,12},{6,14},{8,0},{10,2},{12,4},{14,6},{16,24},{18,... | collective-permute-start | bytes 811016 | tf_op jit(solution)/shard_map/ppermute | solution.py:317
  17.6 2.5 %collective-permute-start.5 = (bf16[2,256,128]{2,1,0:T(8,128)(2,1)S(1)}, bf16[2,256,128]{2,1,0:T(8,128)(2,1)S(1)}, u32[]{:S(2)}, u32[]{:S(2)}) collective-permute-start(bf16[2,256,128]{2,1,0:T(8,128)(2,1)S(1)} %collective-permute-done.3.refs_3_.refs_5_), channel_id=1, source_target_pairs={{0,2},{2,0},{4,6},{6,4},{8,10},{10,8},{12,14},{14,12},{16,18},{18,... | collective-permute-start | bytes 393224 | tf_op jit(solution)/shard_map/ppermute | solution.py:317
  17.6 13.5 %collective-permute-start.6 = (bf16[2,256,128]{2,1,0:T(8,128)(2,1)S(1)}, bf16[2,256,128]{2,1,0:T(8,128)(2,1)S(1)}, u32[]{:S(2)}, u32[]{:S(2)}) collective-permute-start(bf16[2,256,128]{2,1,0:T(8,128)(2,1)S(1)} %collective-permute-done.4.refs_6_), channel_id=1, source_target_pairs={{0,2},{2,0},{4,6},{6,4},{8,10},{10,8},{12,14},{14,12},{16,18},{18,... | collective-permute-start | bytes 393224 | tf_op jit(solution)/shard_map/ppermute | solution.py:317
  34.0 2.6 %collective-permute-start.13 = (bf16[4,256,128]{2,1,0:T(8,128)(2,1)S(1)}, bf16[4,256,128]{2,1,0:T(8,128)(2,1)S(1)}, u32[]{:S(2)}, u32[]{:S(2)}) collective-permute-start(bf16[4,256,128]{2,1,0:T(8,128)(2,1)S(1)} %get-tuple-element.48), channel_id=1, source_target_pairs={{0,2},{2,0},{4,6},{6,4},{8,10},{10,8},{12,14},{14,12},{16,18},{18,... | collective-permute-start | bytes 786440 | tf_op jit(solution)/shard_map/ppermute | solution.py:317
  36.1 6.1 %collective-permute-start.11 = (bf16[4,256,128]{2,1,0:T(8,128)(2,1)S(1)}, bf16[4,256,128]{2,1,0:T(8,128)(2,1)S(1)}, u32[]{:S(2)}, u32[]{:S(2)}) collective-permute-start(bf16[4,256,128]{2,1,0:T(8,128)(2,1)S(1)} %get-tuple-element.44), channel_id=1, source_target_pairs={{0,2},{2,0},{4,6},{6,4},{8,10},{10,8},{12,14},{14,12},{16,18},{18,... | collective-permute-start | bytes 786440 | tf_op jit(solution)/shard_map/ppermute | solution.py:317
  36.7 6.2 %collective-permute-start.14 = (bf16[2,256,128]{2,1,0:T(8,128)(2,1)S(1)}, bf16[2,256,128]{2,1,0:T(8,128)(2,1)S(1)}, u32[]{:S(2)}, u32[]{:S(2)}) collective-permute-start(bf16[2,256,128]{2,1,0:T(8,128)(2,1)S(1)} %get-tuple-element.50), channel_id=1, source_target_pairs={{0,1},{1,0},{2,3},{3,2},{4,5},{5,4},{6,7},{7,6},{8,9},{9,8},{10,11... | collective-permute-start | bytes 393224 | tf_op jit(solution)/shard_map/ppermute | solution.py:321
  36.8 9.9 %collective-permute-start.8 = (bf16[512,128]{1,0:T(8,128)(2,1)S(1)}, bf16[512,128]{1,0:T(8,128)(2,1)S(1)}, u32[]{:S(2)}, u32[]{:S(2)}) collective-permute-start(bf16[512,128]{1,0:T(8,128)(2,1)S(1)} %get-tuple-element.38), channel_id=1, source_target_pairs={{0,4},{2,6},{4,0},{6,2},{8,12},{10,14},{12,8},{14,10},{16,20},{18,... | collective-permute-start | bytes 393224 | tf_op jit(solution)/shard_map/ppermute | solution.py:317
  40.7 8.5 %collective-permute-start.9 = (bf16[512,128]{1,0:T(8,128)(2,1)S(1)}, bf16[512,128]{1,0:T(8,128)(2,1)S(1)}, u32[]{:S(2)}, u32[]{:S(2)}) collective-permute-start(bf16[512,128]{1,0:T(8,128)(2,1)S(1)} %get-tuple-element.39), channel_id=1, source_target_pairs={{0,8},{2,10},{4,12},{6,14},{8,0},{10,2},{12,4},{14,6},{16,24},{18,... | collective-permute-start | bytes 393224 | tf_op jit(solution)/shard_map/ppermute | solution.py:317
  40.7 9.8 %collective-permute-start.10 = (bf16[512,128]{1,0:T(8,128)(2,1)S(1)}, bf16[512,128]{1,0:T(8,128)(2,1)S(1)}, u32[]{:S(2)}, u32[]{:S(2)}) collective-permute-start(bf16[512,128]{1,0:T(8,128)(2,1)S(1)} %get-tuple-element.42), channel_id=1, source_target_pairs={{0,12},{2,14},{4,8},{6,10},{8,4},{10,6},{12,0},{14,2},{16,28},{18,... | collective-permute-start | bytes 393224 | tf_op jit(solution)/shard_map/ppermute | solution.py:317
  42.2 9.1 %collective-permute-start.12 = (bf16[2,256,128]{2,1,0:T(8,128)(2,1)S(1)}, bf16[2,256,128]{2,1,0:T(8,128)(2,1)S(1)}, u32[]{:S(2)}, u32[]{:S(2)}) collective-permute-start(bf16[2,256,128]{2,1,0:T(8,128)(2,1)S(1)} %get-tuple-element.46), channel_id=1, source_target_pairs={{0,1},{1,0},{2,3},{3,2},{4,5},{5,4},{6,7},{7,6},{8,9},{9,8},{10,11... | collective-permute-start | bytes 393224 | tf_op jit(solution)/shard_map/ppermute | solution.py:321
  43.0 8.3 %collective-permute-start.15 = (bf16[2,256,128]{2,1,0:T(8,128)(2,1)S(1)}, bf16[2,256,128]{2,1,0:T(8,128)(2,1)S(1)}, u32[]{:S(2)}, u32[]{:S(2)}) collective-permute-start(bf16[2,256,128]{2,1,0:T(8,128)(2,1)S(1)} %add_convert_fusion), channel_id=1, source_target_pairs={{0,16},{2,18},{4,20},{6,22},{8,24},{10,26},{12,28},{14,30},{16,0},... | collective-permute-start | bytes 393224 | tf_op jit(solution)/shard_map/ppermute | solution.py:317

commit v4 on v3

--- a/solution.py
+++ b/solution.py
@@ -95,13 +95,15 @@
     (order,) = take(1)
     q_in, kv_in = take(len(q_units)), take(n_kv)
     q_before = dict(zip(q_held, take(len(q_held))))
-    k_before = take(1)[0] if k_held else None
+    k_before = take(len(k_held))
     dq_out = dict(zip(q_units, take(len(q_units))))
     sent, kept = take(2) if k_done else (None, take(1)[0])
-    q, g, low, delta, k, v, kt, dqt, total, q_at, k_at, pair_q, pair_k = refs
+    q, g, low, delta, k, v, kt, dqt, *scratch, q_at, k_at, pair_q, pair_k = refs
 
     me = lax.axis_index("blk")
     head = lax.axis_index("head")
+    total = scratch[0] if k_done else kept
+    held_at = {at: (ref, n) for ref, ids in zip(k_before, k_held) for n, at in enumerate(ids)}
     lines = rows // width
     lane = lax.broadcasted_iota(jnp.int32, order.shape, 1)
 
@@ -136,8 +138,9 @@
         half = lax.rem(head + part, 2) if split else part
         k_at[j] = place(2 * (me ^ offset) + half)
         for t in range(2):
-            if blocks[j] in k_held:
-                total[2 * j + t] = k_before[2 * k_held.index(blocks[j]) + t]
+            if blocks[j] in held_at:
+                from_ref, n = held_at[blocks[j]]
+                total[2 * j + t] = from_ref[2 * n + t]
             else:
                 total[2 * j + t] = jnp.zeros((block, width), jnp.float32)
 
@@ -199,8 +202,6 @@
             out[at] = (total[2 * j] * scale).astype(out.dtype)
             out[at + 1] = total[2 * j + 1].astype(out.dtype)
             place[offset & 1] = at + 2
-    else:
-        kept[...] = total[...]
 
 
 def blocks_of(kv):
@@ -233,8 +234,8 @@
         out_shape.append(jax.ShapeDtypeStruct((2 * n_k, block, width), jnp.float32))
     pairs = n_q * n_k // 2
     q_held = tuple(o for o in q_units if o in q_before)
-    k_held, k_before = k_before or ((), None)
-    operands = [*q.values(), *kv, *(q_before[o] for o in q_held)] + ([k_before] if k_held else [])
+    k_held = tuple(ids for ids, _ in k_before)
+    operands = [*q.values(), *kv, *(q_before[o] for o in q_held), *(a for _, a in k_before)]
     shape = (q_units, q_held, q_done, blocks, len(kv), k_held, k_done, skip, split, rows, width, scale)
     outs = pl.pallas_call(
         functools.partial(tile_kernel, shape),
@@ -250,7 +251,7 @@
             pltpu.VMEM((n_k, block, width), jnp.bfloat16),
             pltpu.VMEM((n_k, width, block), jnp.bfloat16),
             pltpu.VMEM((n_q, width, block), jnp.float32),
-            pltpu.VMEM((2 * n_k, block, width), jnp.float32),
+            *[pltpu.VMEM((2 * n_k, block, width), jnp.float32)] * k_done,
             pltpu.SMEM((n_q,), jnp.int32),
             pltpu.SMEM((n_k,), jnp.int32),
             pltpu.SMEM((n_q * n_k + WIDTH,), jnp.int32),
@@ -345,29 +346,35 @@
     tile = functools.partial(tile_grads, order, split=split, rows=rows, scale=scale)
     home_kv, away_kv = some(held, home), some(held, away)
     home_blocks = blocks_of(home_kv)
-    held_q, (total,) = tile(some(q, mine), home_kv, {}, None, (), False)
+    held_q, (total,) = tile(some(q, mine), home_kv, {}, (), (), False)
+    before, skip = [(home_blocks, total)], frozenset()
+    near_kv, near_skip = home_kv, frozenset()
     if split:
         first_kv = {o: arrays[:1] for o, arrays in away_kv.items()}
-        first = q_units[:2]
-        first_blocks = blocks_of(first_kv)
-        more_q, (away_total,) = tile(some(q, first), first_kv, held_q, None, (), False)
+        first, first_blocks = q_units[:2], blocks_of(first_kv)
+        more_q, (total,) = tile(some(q, first), first_kv, held_q, (), (), False)
         held_q |= more_q
-        away_before = (first_blocks, away_total)
-        skip = frozenset((o, at) for o in first for at in first_blocks)
-    else:
-        away_before, skip = None, frozenset()
+        before.append((first_blocks, total))
+        near_kv = home_kv | first_kv
+        near_skip = frozenset((o, at) for o in near[:1] for at in first_blocks)
+        skip = frozenset((o, at) for o in mine + near for at in first_blocks)
     more_q, (total,) = tile(
-        some(q, near), home_kv, some(held_q, held_q.keys() & near), (home_blocks, total), (), False
+        some(q, near),
+        near_kv,
+        some(held_q, held_q.keys() & near),
+        before,
+        (),
+        False,
+        skip=near_skip,
     )
     held_q |= more_q
+    before = [(blocks_of(near_kv), total)]
     dq, (far_sent, far_kept) = tile(
-        some(q, q_units), away_kv, held_q, away_before, mine + near, True, skip=skip
+        some(q, q_units), away_kv, held_q, before, mine + near, True, skip=skip
     )
     held_q = some(dq, late)
     far_got = across(far_sent, 1)
-    last_q, (home_sent, home_kept) = tile(
-        some(q, late), home_kv, held_q, (home_blocks, total), late, True
-    )
+    last_q, (home_sent, home_kept) = tile(some(q, late), home_kv, held_q, before, late, True)
     dq |= last_q
     home_got = across(home_sent, 1)
 

time: 52.2 us -> 47.4 us (0.908)
  waiting for transfers between devices: 17.2 us -> 14.2 us
  starting transfers between devices: 20.2 us -> 17.8 us
  other arithmetic: 0.84 us -> 1.49 us
    ppermute x13, waiting for transfers between devices: 17.2 us -> 10.5 us  [across(): return lax.ppermute(array, 'blk', [(i, i ^ offset) for i in range(devices)])]
    ppermute x3, waiting for transfers between devices: 0.01 us -> 3.68 us  [across_both(): return lax.ppermute(array, ('blk', 'head'), route)]
    ppermute x13, starting transfers between devices: 17.8 us -> 15.1 us  [across(): return lax.ppermute(array, 'blk', [(i, i ^ offset) for i in range(devices)])]
    broadcast_in_dim x1, other arithmetic: 0.01 us -> 0.66 us  [on_device(): order = block_order.astype(jnp.float32)[None]]
  transfers between devices with their start and end apart: 16 -> 16, of which waited for: 5 -> 4; matrix products, arithmetic and copies ran while one was open for 2% -> 3% of each run, Pallas kernels for 15% -> 17%
where the time goes in v4:
time: 47.4 us; the launch traced here: 47.3 us
  starting transfers between devices  17.8 us (38%)
  waiting for transfers between devices  14.2 us (30%)
  Pallas kernels  12.3 us (26%)
  other arithmetic  1.49 us (3%)
  between operations  0.76 us (2%)
  local copies, waits for them, and re-layouts  0.72 us (2%)
    ppermute x13, starting transfers between devices, across(): return lax.ppermute(array, 'blk', [(i, i ^ offset) for i in range(devices)])  15.1 us
    pallas_call x5, Pallas kernels, tile_grads(): pl.pallas_call(functools.partial(tile_kernel, shape), out_shape=out_shape...  10.8 us
    ppermute x13, waiting for transfers between devices, across(): return lax.ppermute(array, 'blk', [(i, i ^ offset) for i in range(devices)])  10.5 us
    ppermute x3, waiting for transfers between devices, across_both(): return lax.ppermute(array, ('blk', 'head'), route)  3.68 us
    ppermute x3, starting transfers between devices, across_both(): return lax.ppermute(array, ('blk', 'head'), route)  2.71 us
    pallas_call x1, Pallas kernels, pack(): pl.pallas_call(functools.partial(pack_kernel, split), out_shape=[jax.Shap...  1.42 us
  transfers between devices with their start and end apart: 16, of which 4 were waited for; matrix products, arithmetic and copies ran while one was open for 3% of the time, Pallas kernels for 17%

profile of v4, /device:TPU:0, one launch (start us, length us, event | category | flops | bytes accessed | tf_op | source)
XLA Modules:
  0.0 47.3 jit_solution(18107287456231179839)
XLA Ops:
  0.6 1.4 %pack.1 = (bf16[1056,128]{1,0:T(8,128)(2,1)S(1)}, bf16[2,256,128]{2,1,0:T(8,128)(2,1)S(1)}, bf16[4,256,128]{2,1,0:T(8,128)(2,1)S(1)}) custom-call(bf16[512,128]{1,0:T(8,128)(2,1)} %refs_0_.1, bf16[512,128]{1,0:T(8,128)(2,1)} %refs_1_.1, bf16[512,128]{1,0:T(8,128)(2,1)} %bitcast.11, bf16[512,128]{1,0:T(8,128)(2,1)} %bitcast.12, bf16[512,128]{1,0:T(8,128)(2,1)} %bitcast.13, ...), custom_call_target="tpu_custom_call" | custom-call | tf_op jit(solution)/shard_map/pack/pallas_call | solution.py:69
  2.1 0.6 %collective-permute-start.7 = (bf16[4,256,128]{2,1,0:T(8,128)(2,1)S(1)}, bf16[4,256,128]{2,1,0:T(8,128)(2,1)S(1)}, u32[]{:S(2)}, u32[]{:S(2)}) collective-permute-start(bf16[4,256,128]{2,1,0:T(8,128)(2,1)S(1)} %get-tuple-element.29.refs_2_.refs_3_), channel_id=1, source_target_pairs={{0,2},{2,0},{4,6},{6,4},{8,10},{10,8},{12,14},{14,12},{16,18},{18,... | collective-permute-start | bytes 786440 | tf_op jit(solution)/shard_map/ppermute | solution.py:318
  2.6 3.7 %collective-permute-start.3 = (bf16[2,256,128]{2,1,0:T(8,128)(2,1)S(1)}, bf16[2,256,128]{2,1,0:T(8,128)(2,1)S(1)}, u32[]{:S(2)}, u32[]{:S(2)}) collective-permute-start(bf16[2,256,128]{2,1,0:T(8,128)(2,1)S(1)} %get-tuple-element.28), channel_id=1, source_target_pairs={{0,16},{2,18},{4,20},{6,22},{8,24},{10,26},{12,28},{14,30},{16,0},... | collective-permute-start | bytes 393224 | tf_op jit(solution)/shard_map/ppermute | solution.py:318
  6.3 1.5 %collective-permute-start = (bf16[1056,128]{1,0:T(8,128)(2,1)S(1)}, bf16[1056,128]{1,0:T(8,128)(2,1)S(1)}, u32[]{:S(2)}, u32[]{:S(2)}) collective-permute-start(bf16[1056,128]{1,0:T(8,128)(2,1)S(1)} %get-tuple-element.27.refs_1_), channel_id=1, source_target_pairs={{0,4},{2,6},{4,0},{6,2},{8,12},{10,14},{12,8},{14,10},{16,20},{18,... | collective-permute-start | bytes 811016 | tf_op jit(solution)/shard_map/ppermute | solution.py:318
  7.8 1.6 %collective-permute-start.1 = (bf16[1056,128]{1,0:T(8,128)(2,1)S(1)}, bf16[1056,128]{1,0:T(8,128)(2,1)S(1)}, u32[]{:S(2)}, u32[]{:S(2)}) collective-permute-start(bf16[1056,128]{1,0:T(8,128)(2,1)S(1)} %get-tuple-element.27.refs_1_), channel_id=1, source_target_pairs={{0,8},{2,10},{4,12},{6,14},{8,0},{10,2},{12,4},{14,6},{16,24},{18,... | collective-permute-start | bytes 811016 | tf_op jit(solution)/shard_map/ppermute | solution.py:318
  9.8 3.5 %collective-permute-done.3.refs_3_.refs_5_ = bf16[2,256,128]{2,1,0:T(8,128)(2,1)S(1)} collective-permute-done((bf16[2,256,128]{2,1,0:T(8,128)(2,1)S(1)}, bf16[2,256,128]{2,1,0:T(8,128)(2,1)S(1)}, u32[]{:S(2)}, u32[]{:S(2)}) %collective-permute-start.3) | collective-permute-done | bytes 131104 | tf_op jit(solution)/shard_map/ppermute | solution.py:318
  13.3 1.6 %collective-permute-start.4 = (bf16[2,256,128]{2,1,0:T(8,128)(2,1)S(1)}, bf16[2,256,128]{2,1,0:T(8,128)(2,1)S(1)}, u32[]{:S(2)}, u32[]{:S(2)}) collective-permute-start(bf16[2,256,128]{2,1,0:T(8,128)(2,1)S(1)} %collective-permute-done.3.refs_3_.refs_5_), channel_id=1, source_target_pairs={{0,1},{1,0},{2,3},{3,2},{4,5},{5,4},{6,7},{7,6},{8,9},{9,8},{10,11... | collective-permute-start | bytes 393224 | tf_op jit(solution)/shard_map/ppermute | solution.py:322
  14.9 0.7 %convert_bitcast_fusion.refs_0_ = f32[1,32]{1,0:T(1,128)S(1)} fusion(s32[32]{0:T(128)} %param.13), kind=kLoop, calls=%fused_computation.5 | loop fusion | flops 32 | bytes 256 | tf_op jit(solution)/shard_map/broadcast_in_dim | solution.py:345
  15.5 3.7 %collective-permute-done.4.refs_6_ = bf16[2,256,128]{2,1,0:T(8,128)(2,1)S(1)} collective-permute-done((bf16[2,256,128]{2,1,0:T(8,128)(2,1)S(1)}, bf16[2,256,128]{2,1,0:T(8,128)(2,1)S(1)}, u32[]{:S(2)}, u32[]{:S(2)}) %collective-permute-start.4) | collective-permute-done | bytes 131104 | tf_op jit(solution)/shard_map/ppermute | solution.py:322
  19.2 1.9 %tile_grads.5 = (f32[2,128,256]{2,1,0:T(8,128)S(1)}, f32[8,256,128]{2,1,0:T(8,128)S(1)}) custom-call(f32[1,32]{1,0:T(1,128)S(1)} %convert_bitcast_fusion.refs_0_, bf16[1056,128]{1,0:T(8,128)(2,1)S(1)} %get-tuple-element.27.refs_1_, bf16[4,256,128]{2,1,0:T(8,128)(2,1)S(1)} %get-tuple-element.29.refs_2_.refs_3_, ...), custom_call_target="tpu_custom_call" | custom-call | flops 335544320 | bytes 1572864 | tf_op jit(solution)/shard_map/tile_grads/pallas_call | solution.py:240
  21.1 1.1 %tile_grads.6 = (f32[2,128,256]{2,1,0:T(8,128)S(1)}, f32[2,128,256]{2,1,0:T(8,128)S(1)}, f32[4,256,128]{2,1,0:T(8,128)S(1)}) custom-call(f32[1,32]{1,0:T(1,128)S(1)} %convert_bitcast_fusion.refs_0_, bf16[1056,128]{1,0:T(8,128)(2,1)S(1)} %get-tuple-element.27.refs_1_, bf16[1056,128]{1,0:T(8,128)(2,1)S(1)} %collective-permute-done.refs_2_.refs_1_, ...), custom_call_target="tpu_custom_call" | custom-call | flops 335544320 | bytes 1572864 | tf_op jit(solution)/shard_map/tile_grads/pallas_call | solution.py:240
  22.2 2.8 %tile_grads.7 = (f32[2,128,256]{2,1,0:T(8,128)S(1)}, f32[2,128,256]{2,1,0:T(8,128)S(1)}, f32[12,256,128]{2,1,0:T(8,128)S(1)}) custom-call(f32[1,32]{1,0:T(1,128)S(1)} %convert_bitcast_fusion.refs_0_, bf16[1056,128]{1,0:T(8,128)(2,1)S(1)} %collective-permute-done.refs_2_.refs_1_, bf16[1056,128]{1,0:T(8,128)(2,1)S(1)} %collective-permute-done.1.refs_2_.refs_3_, ...), custom_call_target="tpu_custom_call" | custom-call | flops 1006632960 | bytes 2621440 | tf_op jit(solution)/shard_map/tile_grads/pallas_call | solution.py:240
  25.1 3.0 %tile_grads.8 = (f32[512,128]{1,0:T(8,128)S(1)}, bf16[512,128]{1,0:T(8,128)(2,1)S(1)}, bf16[512,128]{1,0:T(8,128)(2,1)S(1)}, f32[2,128,256]{2,1,0:T(8,128)S(1)},...) custom-call(f32[1,32]{1,0:T(1,128)S(1)} %convert_bitcast_fusion.refs_0_, ...), custom_call_target="tpu_custom_call" | custom-call | flops 1342177280 | bytes 3145728 | tf_op jit(solution)/shard_map/tile_grads/pallas_call | solution.py:240
  28.2 2.0 %tile_grads.9 = (bf16[512,128]{1,0:T(8,128)(2,1)S(1)}, bf16[4,256,128]{2,1,0:T(8,128)(2,1)S(1)}, f32[4,256,128]{2,1,0:T(8,128)S(1)}) custom-call(f32[1,32]{1,0:T(1,128)S(1)} %convert_bitcast_fusion.refs_0_, bf16[1056,128]{1,0:T(8,128)(2,1)S(1)} %collective-permute-done.2.refs_4_.refs_1_, bf16[4,256,128]{2,1,0:T(8,128)(2,1)S(1)} %get-tuple-element.29.refs_2_.refs_3_, ...), custom_call_target="tpu_custom_call" | custom-call | flops 335544320 | bytes 1572864 | tf_op jit(solution)/shard_map/tile_grads/pallas_call | solution.py:240
  30.1 0.6 %collective-permute-start.11 = (bf16[4,256,128]{2,1,0:T(8,128)(2,1)S(1)}, bf16[4,256,128]{2,1,0:T(8,128)(2,1)S(1)}, u32[]{:S(2)}, u32[]{:S(2)}) collective-permute-start(bf16[4,256,128]{2,1,0:T(8,128)(2,1)S(1)} %get-tuple-element.44), channel_id=1, source_target_pairs={{0,2},{2,0},{4,6},{6,4},{8,10},{10,8},{12,14},{14,12},{16,18},{18,... | collective-permute-start | bytes 786440 | tf_op jit(solution)/shard_map/ppermute | solution.py:318
  30.7 0.8 %collective-permute-start.14 = (bf16[2,256,128]{2,1,0:T(8,128)(2,1)S(1)}, bf16[2,256,128]{2,1,0:T(8,128)(2,1)S(1)}, u32[]{:S(2)}, u32[]{:S(2)}) collective-permute-start(bf16[2,256,128]{2,1,0:T(8,128)(2,1)S(1)} %get-tuple-element.50), channel_id=1, source_target_pairs={{0,1},{1,0},{2,3},{3,2},{4,5},{5,4},{6,7},{7,6},{8,9},{9,8},{10,11... | collective-permute-start | bytes 393224 | tf_op jit(solution)/shard_map/ppermute | solution.py:322
  31.6 0.5 %collective-permute-start.10 = (bf16[512,128]{1,0:T(8,128)(2,1)S(1)}, bf16[512,128]{1,0:T(8,128)(2,1)S(1)}, u32[]{:S(2)}, u32[]{:S(2)}) collective-permute-start(bf16[512,128]{1,0:T(8,128)(2,1)S(1)} %get-tuple-element.42), channel_id=1, source_target_pairs={{0,12},{2,14},{4,8},{6,10},{8,4},{10,6},{12,0},{14,2},{16,28},{18,... | collective-permute-start | bytes 393224 | tf_op jit(solution)/shard_map/ppermute | solution.py:318
  32.1 2.9 %collective-permute-start.8 = (bf16[512,128]{1,0:T(8,128)(2,1)S(1)}, bf16[512,128]{1,0:T(8,128)(2,1)S(1)}, u32[]{:S(2)}, u32[]{:S(2)}) collective-permute-start(bf16[512,128]{1,0:T(8,128)(2,1)S(1)} %get-tuple-element.39), channel_id=1, source_target_pairs={{0,4},{2,6},{4,0},{6,2},{8,12},{10,14},{12,8},{14,10},{16,20},{18,... | collective-permute-start | bytes 393224 | tf_op jit(solution)/shard_map/ppermute | solution.py:318
  35.0 1.5 %collective-permute-start.9 = (bf16[512,128]{1,0:T(8,128)(2,1)S(1)}, bf16[512,128]{1,0:T(8,128)(2,1)S(1)}, u32[]{:S(2)}, u32[]{:S(2)}) collective-permute-start(bf16[512,128]{1,0:T(8,128)(2,1)S(1)} %get-tuple-element.40), channel_id=1, source_target_pairs={{0,8},{2,10},{4,12},{6,14},{8,0},{10,2},{12,4},{14,6},{16,24},{18,... | collective-permute-start | bytes 393224 | tf_op jit(solution)/shard_map/ppermute | solution.py:318
  36.9 1.9 %collective-permute-start.15 = (bf16[2,256,128]{2,1,0:T(8,128)(2,1)S(1)}, bf16[2,256,128]{2,1,0:T(8,128)(2,1)S(1)}, u32[]{:S(2)}, u32[]{:S(2)}) collective-permute-start(bf16[2,256,128]{2,1,0:T(8,128)(2,1)S(1)} %add_convert_fusion), channel_id=1, source_target_pairs={{0,16},{2,18},{4,20},{6,22},{8,24},{10,26},{12,28},{14,30},{16,0},... | collective-permute-start | bytes 393224 | tf_op jit(solution)/shard_map/ppermute | solution.py:318
  38.8 1.8 %collective-permute-done.8 = bf16[512,128]{1,0:T(8,128)(2,1)S(1)} collective-permute-done((bf16[512,128]{1,0:T(8,128)(2,1)S(1)}, bf16[512,128]{1,0:T(8,128)(2,1)S(1)}, u32[]{:S(2)}, u32[]{:S(2)}) %collective-permute-start.8) | collective-permute-done | bytes 131104 | tf_op jit(solution)/shard_map/ppermute | solution.py:318
  40.5 5.2 %collective-permute-done.9 = bf16[512,128]{1,0:T(8,128)(2,1)S(1)} collective-permute-done((bf16[512,128]{1,0:T(8,128)(2,1)S(1)}, bf16[512,128]{1,0:T(8,128)(2,1)S(1)}, u32[]{:S(2)}, u32[]{:S(2)}) %collective-permute-start.9) | collective-permute-done | bytes 131104 | tf_op jit(solution)/shard_map/ppermute | solution.py:318
  45.7 0.8 %add_bitcast_fusion = f32[1,512,128]{2,1,0:T(8,128)} fusion(bf16[512,128]{1,0:T(8,128)(2,1)S(1)} %collective-permute-done.10, bf16[512,128]{1,0:T(8,128)(2,1)S(1)} %collective-permute-done.9, f32[512,128]{1,0:T(8,128)S(1)} %get-tuple-element.38, bf16[512,128]{1,0:T(8,128)(2,1)S(1)} %collective-permute-done.8), kind=kLoop, calls=%fused_computation.2 | loop fusion | flops 393216 | bytes 917504 | tf_op jit(solution)/shard_map/broadcast_in_dim | solution.py:405
  46.5 0.7 %slice_bitcast_fusion = (f32[256,128]{1,0:T(8,128)}, f32[256,128]{1,0:T(8,128)}) fusion(f32[2,256,128]{2,1,0:T(8,128)S(1)} %convert_add_fusion), kind=kLoop, calls=%fused_computation.3 | loop fusion | bytes 524288 | tf_op jit(solution)/shard_map/squeeze | solution.py:390
  (21 shorter events, 1.0 us)
Async XLA Ops:
  2.1 11.2 %collective-permute-start.7 = (bf16[4,256,128]{2,1,0:T(8,128)(2,1)S(1)}, bf16[4,256,128]{2,1,0:T(8,128)(2,1)S(1)}, u32[]{:S(2)}, u32[]{:S(2)}) collective-permute-start(bf16[4,256,128]{2,1,0:T(8,128)(2,1)S(1)} %get-tuple-element.29.refs_2_.refs_3_), channel_id=1, source_target_pairs={{0,2},{2,0},{4,6},{6,4},{8,10},{10,8},{12,14},{14,12},{16,18},{18,... | collective-permute-start | bytes 786440 | tf_op jit(solution)/shard_map/ppermute | solution.py:318
  2.6 10.7 %collective-permute-start.3 = (bf16[2,256,128]{2,1,0:T(8,128)(2,1)S(1)}, bf16[2,256,128]{2,1,0:T(8,128)(2,1)S(1)}, u32[]{:S(2)}, u32[]{:S(2)}) collective-permute-start(bf16[2,256,128]{2,1,0:T(8,128)(2,1)S(1)} %get-tuple-element.28), channel_id=1, source_target_pairs={{0,16},{2,18},{4,20},{6,22},{8,24},{10,26},{12,28},{14,30},{16,0},... | collective-permute-start | bytes 393224 | tf_op jit(solution)/shard_map/ppermute | solution.py:318
  6.3 14.9 %collective-permute-start = (bf16[1056,128]{1,0:T(8,128)(2,1)S(1)}, bf16[1056,128]{1,0:T(8,128)(2,1)S(1)}, u32[]{:S(2)}, u32[]{:S(2)}) collective-permute-start(bf16[1056,128]{1,0:T(8,128)(2,1)S(1)} %get-tuple-element.27.refs_1_), channel_id=1, source_target_pairs={{0,4},{2,6},{4,0},{6,2},{8,12},{10,14},{12,8},{14,10},{16,20},{18,... | collective-permute-start | bytes 811016 | tf_op jit(solution)/shard_map/ppermute | solution.py:318
  7.8 14.5 %collective-permute-start.1 = (bf16[1056,128]{1,0:T(8,128)(2,1)S(1)}, bf16[1056,128]{1,0:T(8,128)(2,1)S(1)}, u32[]{:S(2)}, u32[]{:S(2)}) collective-permute-start(bf16[1056,128]{1,0:T(8,128)(2,1)S(1)} %get-tuple-element.27.refs_1_), channel_id=1, source_target_pairs={{0,8},{2,10},{4,12},{6,14},{8,0},{10,2},{12,4},{14,6},{16,24},{18,... | collective-permute-start | bytes 811016 | tf_op jit(solution)/shard_map/ppermute | solution.py:318
  9.3 15.8 %collective-permute-start.2 = (bf16[1056,128]{1,0:T(8,128)(2,1)S(1)}, bf16[1056,128]{1,0:T(8,128)(2,1)S(1)}, u32[]{:S(2)}, u32[]{:S(2)}) collective-permute-start(bf16[1056,128]{1,0:T(8,128)(2,1)S(1)} %get-tuple-element.27.refs_1_), channel_id=1, source_target_pairs={{0,12},{2,14},{4,8},{6,10},{8,4},{10,6},{12,0},{14,2},{16,28},{18,... | collective-permute-start | bytes 811016 | tf_op jit(solution)/shard_map/ppermute | solution.py:318
  13.3 7.9 %collective-permute-start.5 = (bf16[2,256,128]{2,1,0:T(8,128)(2,1)S(1)}, bf16[2,256,128]{2,1,0:T(8,128)(2,1)S(1)}, u32[]{:S(2)}, u32[]{:S(2)}) collective-permute-start(bf16[2,256,128]{2,1,0:T(8,128)(2,1)S(1)} %collective-permute-done.3.refs_3_.refs_5_), channel_id=1, source_target_pairs={{0,2},{2,0},{4,6},{6,4},{8,10},{10,8},{12,14},{14,12},{16,18},{18,... | collective-permute-start | bytes 393224 | tf_op jit(solution)/shard_map/ppermute | solution.py:318
  13.3 5.9 %collective-permute-start.4 = (bf16[2,256,128]{2,1,0:T(8,128)(2,1)S(1)}, bf16[2,256,128]{2,1,0:T(8,128)(2,1)S(1)}, u32[]{:S(2)}, u32[]{:S(2)}) collective-permute-start(bf16[2,256,128]{2,1,0:T(8,128)(2,1)S(1)} %collective-permute-done.3.refs_3_.refs_5_), channel_id=1, source_target_pairs={{0,1},{1,0},{2,3},{3,2},{4,5},{5,4},{6,7},{7,6},{8,9},{9,8},{10,11... | collective-permute-start | bytes 393224 | tf_op jit(solution)/shard_map/ppermute | solution.py:322
  19.2 5.9 %collective-permute-start.6 = (bf16[2,256,128]{2,1,0:T(8,128)(2,1)S(1)}, bf16[2,256,128]{2,1,0:T(8,128)(2,1)S(1)}, u32[]{:S(2)}, u32[]{:S(2)}) collective-permute-start(bf16[2,256,128]{2,1,0:T(8,128)(2,1)S(1)} %collective-permute-done.4.refs_6_), channel_id=1, source_target_pairs={{0,2},{2,0},{4,6},{6,4},{8,10},{10,8},{12,14},{14,12},{16,18},{18,... | collective-permute-start | bytes 393224 | tf_op jit(solution)/shard_map/ppermute | solution.py:318
  28.1 2.6 %collective-permute-start.13 = (bf16[4,256,128]{2,1,0:T(8,128)(2,1)S(1)}, bf16[4,256,128]{2,1,0:T(8,128)(2,1)S(1)}, u32[]{:S(2)}, u32[]{:S(2)}) collective-permute-start(bf16[4,256,128]{2,1,0:T(8,128)(2,1)S(1)} %get-tuple-element.48), channel_id=1, source_target_pairs={{0,2},{2,0},{4,6},{6,4},{8,10},{10,8},{12,14},{14,12},{16,18},{18,... | collective-permute-start | bytes 786440 | tf_op jit(solution)/shard_map/ppermute | solution.py:318
  30.1 6.4 %collective-permute-start.11 = (bf16[4,256,128]{2,1,0:T(8,128)(2,1)S(1)}, bf16[4,256,128]{2,1,0:T(8,128)(2,1)S(1)}, u32[]{:S(2)}, u32[]{:S(2)}) collective-permute-start(bf16[4,256,128]{2,1,0:T(8,128)(2,1)S(1)} %get-tuple-element.44), channel_id=1, source_target_pairs={{0,2},{2,0},{4,6},{6,4},{8,10},{10,8},{12,14},{14,12},{16,18},{18,... | collective-permute-start | bytes 786440 | tf_op jit(solution)/shard_map/ppermute | solution.py:318
  30.7 6.1 %collective-permute-start.14 = (bf16[2,256,128]{2,1,0:T(8,128)(2,1)S(1)}, bf16[2,256,128]{2,1,0:T(8,128)(2,1)S(1)}, u32[]{:S(2)}, u32[]{:S(2)}) collective-permute-start(bf16[2,256,128]{2,1,0:T(8,128)(2,1)S(1)} %get-tuple-element.50), channel_id=1, source_target_pairs={{0,1},{1,0},{2,3},{3,2},{4,5},{5,4},{6,7},{7,6},{8,9},{9,8},{10,11... | collective-permute-start | bytes 393224 | tf_op jit(solution)/shard_map/ppermute | solution.py:322
  31.6 7.2 %collective-permute-start.10 = (bf16[512,128]{1,0:T(8,128)(2,1)S(1)}, bf16[512,128]{1,0:T(8,128)(2,1)S(1)}, u32[]{:S(2)}, u32[]{:S(2)}) collective-permute-start(bf16[512,128]{1,0:T(8,128)(2,1)S(1)} %get-tuple-element.42), channel_id=1, source_target_pairs={{0,12},{2,14},{4,8},{6,10},{8,4},{10,6},{12,0},{14,2},{16,28},{18,... | collective-permute-start | bytes 393224 | tf_op jit(solution)/shard_map/ppermute | solution.py:318
  32.1 8.4 %collective-permute-start.8 = (bf16[512,128]{1,0:T(8,128)(2,1)S(1)}, bf16[512,128]{1,0:T(8,128)(2,1)S(1)}, u32[]{:S(2)}, u32[]{:S(2)}) collective-permute-start(bf16[512,128]{1,0:T(8,128)(2,1)S(1)} %get-tuple-element.39), channel_id=1, source_target_pairs={{0,4},{2,6},{4,0},{6,2},{8,12},{10,14},{12,8},{14,10},{16,20},{18,... | collective-permute-start | bytes 393224 | tf_op jit(solution)/shard_map/ppermute | solution.py:318
  35.0 10.7 %collective-permute-start.9 = (bf16[512,128]{1,0:T(8,128)(2,1)S(1)}, bf16[512,128]{1,0:T(8,128)(2,1)S(1)}, u32[]{:S(2)}, u32[]{:S(2)}) collective-permute-start(bf16[512,128]{1,0:T(8,128)(2,1)S(1)} %get-tuple-element.40), channel_id=1, source_target_pairs={{0,8},{2,10},{4,12},{6,14},{8,0},{10,2},{12,4},{14,6},{16,24},{18,... | collective-permute-start | bytes 393224 | tf_op jit(solution)/shard_map/ppermute | solution.py:318
  36.5 10.0 %collective-permute-start.12 = (bf16[2,256,128]{2,1,0:T(8,128)(2,1)S(1)}, bf16[2,256,128]{2,1,0:T(8,128)(2,1)S(1)}, u32[]{:S(2)}, u32[]{:S(2)}) collective-permute-start(bf16[2,256,128]{2,1,0:T(8,128)(2,1)S(1)} %get-tuple-element.46), channel_id=1, source_target_pairs={{0,1},{1,0},{2,3},{3,2},{4,5},{5,4},{6,7},{7,6},{8,9},{9,8},{10,11... | collective-permute-start | bytes 393224 | tf_op jit(solution)/shard_map/ppermute | solution.py:322
  36.9 9.6 %collective-permute-start.15 = (bf16[2,256,128]{2,1,0:T(8,128)(2,1)S(1)}, bf16[2,256,128]{2,1,0:T(8,128)(2,1)S(1)}, u32[]{:S(2)}, u32[]{:S(2)}) collective-permute-start(bf16[2,256,128]{2,1,0:T(8,128)(2,1)S(1)} %add_convert_fusion), channel_id=1, source_target_pairs={{0,16},{2,18},{4,20},{6,22},{8,24},{10,26},{12,28},{14,30},{16,0},... | collective-permute-start | bytes 393224 | tf_op jit(solution)/shard_map/ppermute | solution.py:318
